TPU v7x, 32 devices: a whole 2x2x4 slice. The times are simulated.
32 devices in a mesh: dp: 2 (over x), tp: 4 (over z), ctx: 4 (over y, core).
Axes of the slice: x: 2, y: 2, z: 4, core: 2. Of those that a mesh axis runs over, the one named last changes fastest.
Arguments:
- x_tokens: bfloat16 [2048, 5120], P(('dp', 'ctx')), parts along dimension 0
- positions: int32 [2048], P(('dp', 'ctx')), parts along dimension 0
- w_dq: bfloat16 [5120, 1536], replicated
- g_q: bfloat16 [1536], replicated
- w_uq: bfloat16 [1536, 16384], P(None, 'tp')
- w_qr: bfloat16 [1536, 8192], P(None, 'tp')
- w_dkv: bfloat16 [5120, 512], replicated
- g_kv: bfloat16 [512], replicated
- w_kr: bfloat16 [5120, 64], replicated
- w_uk: bfloat16 [512, 16384], P(None, 'tp')
- w_uv: bfloat16 [512, 16384], P(None, 'tp')
- w_o: bfloat16 [16384, 5120], P('tp')
Outputs:
- output: bfloat16 [2048, 5120], P(('dp', 'ctx')), parts along dimension 0
There are 2 independent parts. A program takes and returns all parts, laid end to end along the dimension named above; an argument that names none is the same for every part.
All inputs are finite; a program needn't handle non-finite values.
Results may differ from a plain program's by a relative error of at most 0.00853476.
Values are sent between devices in bfloat16 or wider.
A program may use at most 1 GiB of HBM per device.

v0:
```python
import jax
import jax.numpy as jnp
from jax import lax
from jax.sharding import PartitionSpec as P

ROPE_BASE = 10000.0
NORM_EPS = 1e-6
NEG_BIG = -1e30


def rms_norm(act_in, gain_vec):
    inv_rms = lax.rsqrt(jnp.mean(act_in * act_in, axis=-1, keepdims=True) + NORM_EPS)
    return act_in * inv_rms * gain_vec.astype(jnp.float32)


def rope_tables(pos_vals, rope_dim):
    half_dim = rope_dim // 2
    inv_freq = ROPE_BASE ** (-jnp.arange(half_dim, dtype=jnp.float32) * 2.0 / rope_dim)
    angles = pos_vals.astype(jnp.float32)[..., None] * inv_freq
    return jnp.cos(angles), jnp.sin(angles)


def apply_rope(act_in, cos_t, sin_t):
    half_dim = act_in.shape[-1] // 2
    first_half = act_in[..., :half_dim]
    second_half = act_in[..., half_dim:]
    return jnp.concatenate([first_half * cos_t - second_half * sin_t, second_half * cos_t + first_half * sin_t], axis=-1)


def project_tokens(tok_x, tok_pos, w_dq, g_q, w_uq, w_qr, w_dkv, g_kv, w_kr, heads_loc):
    rope_dim = w_kr.shape[1]
    tok_count = tok_x.shape[0]
    cos_t, sin_t = rope_tables(tok_pos, rope_dim)
    c_q = rms_norm(jnp.dot(tok_x, w_dq, preferred_element_type=jnp.float32), g_q).astype(jnp.bfloat16)
    q_nope = jnp.dot(c_q, w_uq, preferred_element_type=jnp.float32).astype(jnp.bfloat16).reshape(tok_count, heads_loc, -1)
    q_rot = jnp.dot(c_q, w_qr, preferred_element_type=jnp.float32).reshape(tok_count, heads_loc, rope_dim)
    q_pe = apply_rope(q_rot, cos_t[:, None, :], sin_t[:, None, :]).astype(jnp.bfloat16)
    c_kv = rms_norm(jnp.dot(tok_x, w_dkv, preferred_element_type=jnp.float32), g_kv).astype(jnp.bfloat16)
    k_pe = apply_rope(jnp.dot(tok_x, w_kr, preferred_element_type=jnp.float32), cos_t, sin_t).astype(jnp.bfloat16)
    return q_nope, q_pe, c_kv, k_pe


def up_project(lat_rows, w_uk, w_uv, heads_loc):
    row_count = lat_rows.shape[0]
    k_nope = jnp.dot(lat_rows, w_uk, preferred_element_type=jnp.float32).astype(jnp.bfloat16).reshape(row_count, heads_loc, -1)
    v_rows = jnp.dot(lat_rows, w_uv, preferred_element_type=jnp.float32).astype(jnp.bfloat16).reshape(row_count, heads_loc, -1)
    return k_nope, v_rows


def block_scores(q_nope, q_pe, k_nope, k_pe, score_scale):
    nope_part = jnp.einsum('qhn,khn->hqk', q_nope, k_nope, preferred_element_type=jnp.float32)
    rope_part = jnp.einsum('qhr,kr->hqk', q_pe, k_pe, preferred_element_type=jnp.float32)
    return (nope_part + rope_part) * score_scale


def block_stats(scores, v_rows):
    blk_max = jnp.max(scores, axis=-1)
    prob_tile = jnp.exp(scores - blk_max[..., None])
    blk_sum = jnp.sum(prob_tile, axis=-1)
    blk_acc = jnp.einsum('hqk,khv->hqv', prob_tile.astype(jnp.bfloat16), v_rows, preferred_element_type=jnp.float32)
    return blk_max, blk_sum, blk_acc


def merge_stats(run_state, update):
    old_max, old_sum, old_acc = run_state
    new_max, new_sum, new_acc = update
    top_max = jnp.maximum(old_max, new_max)
    old_w = jnp.exp(old_max - top_max)
    new_w = jnp.exp(new_max - top_max)
    return top_max, old_sum * old_w + new_sum * new_w, old_acc * old_w[..., None] + new_acc * new_w[..., None]


def solution(mesh):
    ctx_count = mesh.shape['ctx']
    next_perm = [(src, (src + 1) % ctx_count) for src in range(ctx_count)]
    tok_spec = P(('dp', 'ctx'), None)
    pos_spec = P(('dp', 'ctx'))
    full_mat = P(None, None)
    full_vec = P(None)
    col_spec = P(None, 'tp')
    row_spec = P('tp', None)

    def local_step(tok_x, tok_pos, w_dq, g_q, w_uq, w_qr, w_dkv, g_kv, w_kr, w_uk, w_uv, w_o):
        my_index = lax.axis_index('ctx')
        half_len = tok_x.shape[0] // 2
        rope_dim = w_kr.shape[1]
        heads_loc = w_qr.shape[1] // rope_dim
        nope_dim = w_uq.shape[1] // heads_loc
        value_dim = w_uv.shape[1] // heads_loc
        score_scale = (nope_dim + rope_dim) ** -0.5
        q_nope, q_pe, c_kv, k_pe = project_tokens(tok_x, tok_pos, w_dq, g_q, w_uq, w_qr, w_dkv, g_kv, w_kr, heads_loc)
        k_nope, v_rows = up_project(c_kv, w_uk, w_uv, heads_loc)
        scores = block_scores(q_nope, q_pe, k_nope, k_pe, score_scale)
        visible = tok_pos[None, :] <= tok_pos[:, None]
        run_state = block_stats(jnp.where(visible[None], scores, NEG_BIG), v_rows)

        def attend_lower(lat_blk, rot_blk, run_state):
            k_low, v_low = up_project(lat_blk[:half_len], w_uk, w_uv, heads_loc)
            update = block_stats(block_scores(q_nope, q_pe, k_low, rot_blk[:half_len], score_scale), v_low)
            return merge_stats(run_state, update)

        def attend_upper(lat_blk, rot_blk, run_state):
            k_both, v_both = up_project(lat_blk, w_uk, w_uv, heads_loc)
            update = block_stats(block_scores(q_nope[half_len:], q_pe[half_len:], k_both, rot_blk, score_scale), v_both)
            old_max, old_sum, old_acc = run_state
            top_max, top_sum, top_acc = merge_stats((old_max[:, half_len:], old_sum[:, half_len:], old_acc[:, half_len:]), update)
            return (jnp.concatenate([old_max[:, :half_len], top_max], axis=1),
                    jnp.concatenate([old_sum[:, :half_len], top_sum], axis=1),
                    jnp.concatenate([old_acc[:, :half_len], top_acc], axis=1))

        def ctx_step(hop_idx, loop_carry):
            lat_blk, rot_blk, run_state = loop_carry
            lat_blk = lax.ppermute(lat_blk, 'ctx', next_perm)
            rot_blk = lax.ppermute(rot_blk, 'ctx', next_perm)
            src_index = (my_index - hop_idx) % ctx_count
            run_state = lax.cond(src_index < my_index, attend_lower, attend_upper, lat_blk, rot_blk, run_state)
            return lat_blk, rot_blk, run_state

        loop_carry = lax.fori_loop(1, ctx_count, ctx_step, (c_kv, k_pe, run_state))
        run_max, run_sum, run_acc = loop_carry[2]
        attn_out = (run_acc / run_sum[..., None]).astype(jnp.bfloat16)
        y_part = jnp.einsum('htv,hvd->td', attn_out, w_o.reshape(heads_loc, value_dim, -1), preferred_element_type=jnp.float32)
        return lax.psum(y_part, 'tp').astype(jnp.bfloat16)

    return jax.shard_map(local_step, mesh=mesh,
                         in_specs=(tok_spec, pos_spec, full_mat, full_vec, col_spec, col_spec, full_mat, full_vec, full_mat, col_spec, col_spec, row_spec),
                         out_specs=tok_spec, check_vma=False)
```

profile of v0, /device:TPU:0, one launch (start us, length us, event | category | flops | bytes accessed | tf_op | source)
XLA Modules:
  0.0 312.4 jit_solution(17838471273733439101)
XLA Ops:
  1.7 7.8 %multiply_reduce_fusion = (f32[256]{0:T(256)S(1)}, f32[256,1536]{1,0:T(8,128)S(1)}) fusion(bf16[256,5120]{1,0:T(8,128)(2,1)S(1)} %copy-done, bf16[5120,1536]{1,0:T(8,128)(2,1)} %param.18), kind=kOutput, calls=%fused_computation.74 | convolution fusion | flops 4027318016 | bytes 19923968 | tf_op jit(solution)/shard_map/dot_general | solution.py:34
  9.6 5.7 %fusion.53 = f32[256,2048]{0,1:T(8,128)S(1)} fusion(bf16[1536,2048]{1,0:T(8,128)(2,1)} %param.21, f32[256,1536]{1,0:T(8,128)S(1)} %get-tuple-element.416, f32[1536]{0:T(1024)S(1)} %convert_element_type.66, f32[256]{0:T(256)S(1)} %add_rsqrt_fusion), kind=kOutput, calls=%fused_computation.90 | convolution fusion | flops 1611792384 | bytes 9968640 | tf_op jit(solution)/shard_map/dot_general | solution.py:36
  17.0 4.1 %fusion.49 = bf16[32,32,8,128]{3,2,1,0:T(8,128)(2,1)S(1)} fusion(bf16[1536,4096]{1,0:T(8,128)(2,1)S(1)} %copy-done.13, f32[256,1536]{1,0:T(8,128)S(1)} %get-tuple-element.416, f32[1536]{0:T(1024)S(1)} %convert_element_type.66, f32[256]{0:T(256)S(1)} %add_rsqrt_fusion), kind=kOutput, calls=%fused_computation.70 | convolution fusion | flops 3223453696 | bytes 16260096 | tf_op jit(solution)/shard_map/dot_general | solution.py:35
  29.5 3.8 %fusion.40 = f32[32,256,128]{2,1,0:T(8,128)} fusion(f32[32,256,256]{1,2,0:T(8,128)S(1)} %get-tuple-element.418, f32[32,256]{1,0:T(8,128)S(1)} %get-tuple-element.501, bf16[32,32,8,128]{3,2,1,0:T(8,128)(2,1)S(1)} %fusion.51), kind=kOutput, calls=%fused_computation.60 | convolution fusion | flops 541065216 | bytes 14712832 | tf_op jit(solution)/shard_map/hqk,khv->hqv/dot_general | solution.py:60
  37.9 70.4 %while.23 = (s32[]{:T(128)}, bf16[256,512]{1,0:T(8,128)(2,1)S(1)}, bf16[256,64]{0,1:T(8,128)(2,1)S(1)}, f32[32,256]{1,0:T(8,128)S(1)}, f32[32,256]{1,0:T(8,128)S...) while((s32[]{:T(128)}, bf16[256,512]{1,0:T(8,128)(2,1)S(1)}, ...), condition=%wide.region_11.12_spmd, body=%wide.region_4.11_spmd.sunk | while | flops 2830663680 | bytes 97927776 | solution.py:119
  38.4 2.6 collective-permute-start.1
  41.1 3.7 %collective-permute-done.1 = bf16[256,64]{0,1:T(8,128)(2,1)S(1)} collective-permute-done((bf16[256,64]{0,1:T(8,128)(2,1)S(1)}, bf16[256,64]{0,1:T(8,128)(2,1)S(1)}, u32[]{:S(2)}, u32[]{:S(2)}) %collective-permute-start.1) | collective-permute-done | bytes 32800 | tf_op jit(solution)/shard_map/while/body/eval_jaxpr/ppermute | solution.py:114
  44.8 17.0 %conditional.2 = (f32[32,256]{1,0:T(8,128)S(1)}, f32[32,256]{1,0:T(8,128)S(1)}, f32[32,256,128]{2,1,0:T(8,128)}) conditional(s32[]{:T(128)} %convert_element_type.110, (f32[32,256]{1,0:T(8,128)S(1)}, bf16[256,512]{1,0:T(8,128)(2,1)S(1)}, bf16[512,4096]{1,0:T(8,128)(2,1)}, bf16[256,32,128]{2,0,1:T(8,128)(2,1)}, bf16[256,32,64]{0,2,1:T(8,128)(2,1)}, ...), branch_computations={%region_5.7_spmd, %region_8.10_spmd} | conditional | flops 2830663680 | bytes 96157808 | solution.py:116
  44.8 3.5 %fusion.10 = bf16[32,32,8,128]{3,2,1,0:T(8,128)(2,1)S(1)} fusion(bf16[256,512]{1,0:T(8,128)(2,1)S(1)} %get-tuple-element.309, bf16[512,4096]{1,0:T(8,128)(2,1)} %get-tuple-element.310), kind=kOutput, calls=%fused_computation.15 | convolution fusion | flops 1074790400 | bytes 6553600 | tf_op jit(solution)/shard_map/while/body/eval_jaxpr/cond/branch_0_fun/dot_general | solution.py:45
  56.4 2.7 multiply_add_fusion
  59.4 2.4 pad_maximum_fusion
  62.2 2.5 collective-permute-start.1
  64.7 3.3 %collective-permute-done.1 = bf16[256,64]{0,1:T(8,128)(2,1)S(1)} collective-permute-done((bf16[256,64]{0,1:T(8,128)(2,1)S(1)}, bf16[256,64]{0,1:T(8,128)(2,1)S(1)}, u32[]{:S(2)}, u32[]{:S(2)}) %collective-permute-start.1) | collective-permute-done | bytes 32800 | tf_op jit(solution)/shard_map/while/body/eval_jaxpr/ppermute | solution.py:114
  68.1 17.0 %conditional.2 = (f32[32,256]{1,0:T(8,128)S(1)}, f32[32,256]{1,0:T(8,128)S(1)}, f32[32,256,128]{2,1,0:T(8,128)}) conditional(s32[]{:T(128)} %convert_element_type.110, (f32[32,256]{1,0:T(8,128)S(1)}, bf16[256,512]{1,0:T(8,128)(2,1)S(1)}, bf16[512,4096]{1,0:T(8,128)(2,1)}, bf16[256,32,128]{2,0,1:T(8,128)(2,1)}, bf16[256,32,64]{0,2,1:T(8,128)(2,1)}, ...), branch_computations={%region_5.7_spmd, %region_8.10_spmd} | conditional | flops 2830663680 | bytes 96157808 | solution.py:116
  68.1 3.5 %fusion.10 = bf16[32,32,8,128]{3,2,1,0:T(8,128)(2,1)S(1)} fusion(bf16[256,512]{1,0:T(8,128)(2,1)S(1)} %get-tuple-element.309, bf16[512,4096]{1,0:T(8,128)(2,1)} %get-tuple-element.310), kind=kOutput, calls=%fused_computation.15 | convolution fusion | flops 1074790400 | bytes 6553600 | tf_op jit(solution)/shard_map/while/body/eval_jaxpr/cond/branch_0_fun/dot_general | solution.py:45
  79.7 2.7 multiply_add_fusion
  82.7 2.4 pad_maximum_fusion
  85.5 2.9 collective-permute-start.1
  88.4 2.9 collective-permute-done.1
  91.3 17.0 %conditional.2 = (f32[32,256]{1,0:T(8,128)S(1)}, f32[32,256]{1,0:T(8,128)S(1)}, f32[32,256,128]{2,1,0:T(8,128)}) conditional(s32[]{:T(128)} %convert_element_type.110, (f32[32,256]{1,0:T(8,128)S(1)}, bf16[256,512]{1,0:T(8,128)(2,1)S(1)}, bf16[512,4096]{1,0:T(8,128)(2,1)}, bf16[256,32,128]{2,0,1:T(8,128)(2,1)}, bf16[256,32,64]{0,2,1:T(8,128)(2,1)}, ...), branch_computations={%region_5.7_spmd, %region_8.10_spmd} | conditional | flops 2830663680 | bytes 96157808 | solution.py:116
  91.3 3.5 %fusion.10 = bf16[32,32,8,128]{3,2,1,0:T(8,128)(2,1)S(1)} fusion(bf16[256,512]{1,0:T(8,128)(2,1)S(1)} %get-tuple-element.309, bf16[512,4096]{1,0:T(8,128)(2,1)} %get-tuple-element.310), kind=kOutput, calls=%fused_computation.15 | convolution fusion | flops 1074790400 | bytes 6553600 | tf_op jit(solution)/shard_map/while/body/eval_jaxpr/cond/branch_0_fun/dot_general | solution.py:45
  103.0 2.7 multiply_add_fusion
  108.4 21.7 %convolution_bitcast_fusion = f32[256,5120]{1,0:T(8,128)} fusion(bf16[32,128,5120]{2,1,0:T(8,128)(2,1)} %bitcast.97, f32[32,256,128]{2,1,0:T(8,128)} %get-tuple-element.343, f32[32,256]{1,0:T(8,128)S(1)} %get-tuple-element.344), kind=kOutput, calls=%fused_computation.56 | convolution fusion | flops 10739515392 | bytes 51412992 | tf_op jit(solution)/shard_map/htv,hvd->td/dot_general | solution.py:122
  130.1 182.3 %all-reduce.1 = bf16[256,5120]{1,0:T(8,128)(2,1)} all-reduce(f32[256,5120]{1,0:T(8,128)} %convolution_bitcast_fusion), channel_id=1, replica_groups=mesh['dp'=2,'tp'=4,'ctx'=4] {'tp'}, use_global_device_ids=true, to_apply=%region_12.13 | all-reduce | flops 1310720 | bytes 7864320 | tf_op jit(solution)/shard_map/psum | solution.py:123
  (89 shorter events, 45.1 us)
Async XLA Ops:
  0.0 1.7 copy-start
  0.0 9.6 %copy-start.11 = (bf16[1536]{0:T(1024)(128)(2,1)S(1)}, bf16[1536]{0:T(1024)(128)(2,1)}, u32[]{:S(2)}) copy-start(bf16[1536]{0:T(1024)(128)(2,1)} %param.19) | copy-start | bytes 9220
  9.6 5.8 %copy-start.9 = (bf16[5120,64]{0,1:T(8,128)(2,1)S(1)}, bf16[5120,64]{0,1:T(8,128)(2,1)}, u32[]{:S(2)}) copy-start(bf16[5120,64]{0,1:T(8,128)(2,1)} %param.24) | copy-start | bytes 1966084
  9.6 6.7 %copy-start.10 = (s32[256]{0:T(256)S(1)}, s32[256]{0:T(256)}, u32[]{:S(2)}) copy-start(s32[256]{0:T(256)} %param.17) | copy-start | bytes 3076
  9.6 7.3 %copy-start.13 = (bf16[1536,4096]{1,0:T(8,128)(2,1)S(1)}, bf16[1536,4096]{1,0:T(8,128)(2,1)}, u32[]{:S(2)}) copy-start(bf16[1536,4096]{1,0:T(8,128)(2,1)} %param.20) | copy-start | bytes 37748740
  16.5 4.5 %slice-start = ((s8[5242880]{0:T(1024)(128)(4,1)}), s8[1048576]{0:T(1024)(128)(4,1)S(1)}, s32[]{:S(2)}) async-start(s8[5242880]{0:T(1024)(128)(4,1)} %bitcast.98), calls=%async_computation | async-start | bytes 2097152
  16.9 4.1 %slice-start.1 = ((s8[5242880]{0:T(1024)(128)(4,1)}), s8[4194304]{0:T(1024)(128)(4,1)S(1)}, s32[]{:S(2)}) async-start(s8[5242880]{0:T(1024)(128)(4,1)} %bitcast.98), calls=%async_computation.1 | async-start | bytes 8388608
  21.1 1.6 copy-start.12
  21.1 2.2 copy-start.5
  26.0 2.2 copy-start.6
  37.9 6.9 %collective-permute-start = (bf16[256,512]{1,0:T(8,128)(2,1)S(1)}, bf16[256,512]{1,0:T(8,128)(2,1)S(1)}, u32[]{:S(2)}, u32[]{:S(2)}) collective-permute-start(bf16[256,512]{1,0:T(8,128)(2,1)S(1)} %get-tuple-element.514), channel_id=1, source_target_pairs={{0,1},{1,2},{2,3},{3,0},{4,5},{5,6},{6,7},{7,4},{8,9},{9,10},{10,1... | collective-permute-start | bytes 786440 | tf_op jit(solution)/shard_map/while/body/eval_jaxpr/ppermute | solution.py:113
  38.4 6.4 %collective-permute-start.1 = (bf16[256,64]{0,1:T(8,128)(2,1)S(1)}, bf16[256,64]{0,1:T(8,128)(2,1)S(1)}, u32[]{:S(2)}, u32[]{:S(2)}) collective-permute-start(bf16[256,64]{0,1:T(8,128)(2,1)S(1)} %get-tuple-element.515), channel_id=1, source_target_pairs={{0,1},{1,2},{2,3},{3,0},{4,5},{5,6},{6,7},{7,4},{8,9},{9,10},{10,1... | collective-permute-start | bytes 98312 | tf_op jit(solution)/shard_map/while/body/eval_jaxpr/ppermute | solution.py:114
  52.1 2.2 copy-start.7
  54.3 2.2 copy-start.2
  61.8 6.2 %collective-permute-start = (bf16[256,512]{1,0:T(8,128)(2,1)S(1)}, bf16[256,512]{1,0:T(8,128)(2,1)S(1)}, u32[]{:S(2)}, u32[]{:S(2)}) collective-permute-start(bf16[256,512]{1,0:T(8,128)(2,1)S(1)} %get-tuple-element.514), channel_id=1, source_target_pairs={{0,1},{1,2},{2,3},{3,0},{4,5},{5,6},{6,7},{7,4},{8,9},{9,10},{10,1... | collective-permute-start | bytes 786440 | tf_op jit(solution)/shard_map/while/body/eval_jaxpr/ppermute | solution.py:113
  62.2 5.8 %collective-permute-start.1 = (bf16[256,64]{0,1:T(8,128)(2,1)S(1)}, bf16[256,64]{0,1:T(8,128)(2,1)S(1)}, u32[]{:S(2)}, u32[]{:S(2)}) collective-permute-start(bf16[256,64]{0,1:T(8,128)(2,1)S(1)} %get-tuple-element.515), channel_id=1, source_target_pairs={{0,1},{1,2},{2,3},{3,0},{4,5},{5,6},{6,7},{7,4},{8,9},{9,10},{10,1... | collective-permute-start | bytes 98312 | tf_op jit(solution)/shard_map/while/body/eval_jaxpr/ppermute | solution.py:114
  75.3 2.2 copy-start.7
  77.5 2.2 copy-start.2
  85.1 6.2 %collective-permute-start = (bf16[256,512]{1,0:T(8,128)(2,1)S(1)}, bf16[256,512]{1,0:T(8,128)(2,1)S(1)}, u32[]{:S(2)}, u32[]{:S(2)}) collective-permute-start(bf16[256,512]{1,0:T(8,128)(2,1)S(1)} %get-tuple-element.514), channel_id=1, source_target_pairs={{0,1},{1,2},{2,3},{3,0},{4,5},{5,6},{6,7},{7,4},{8,9},{9,10},{10,1... | collective-permute-start | bytes 786440 | tf_op jit(solution)/shard_map/while/body/eval_jaxpr/ppermute | solution.py:113
  85.5 5.8 %collective-permute-start.1 = (bf16[256,64]{0,1:T(8,128)(2,1)S(1)}, bf16[256,64]{0,1:T(8,128)(2,1)S(1)}, u32[]{:S(2)}, u32[]{:S(2)}) collective-permute-start(bf16[256,64]{0,1:T(8,128)(2,1)S(1)} %get-tuple-element.515), channel_id=1, source_target_pairs={{0,1},{1,2},{2,3},{3,0},{4,5},{5,6},{6,7},{7,4},{8,9},{9,10},{10,1... | collective-permute-start | bytes 98312 | tf_op jit(solution)/shard_map/while/body/eval_jaxpr/ppermute | solution.py:114
  98.6 2.2 copy-start.7
  100.8 2.2 copy-start.2
  108.4 204.0 %copy-start.1 = (bf16[256,5120]{1,0:T(8,128)(2,1)S(1)}, bf16[256,5120]{1,0:T(8,128)(2,1)}, u32[]{:S(2)}) copy-start(bf16[256,5120]{1,0:T(8,128)(2,1)} %param.16) | copy-start | bytes 7864324
where the time goes:
time: 313 us; the launch traced here: 312 us
  blocking collectives  182 us (58%)
  matrix products  85.4 us (27%)
  other arithmetic  13.1 us (4%)
  local copies, waits for them, and re-layouts  11.9 us (4%)
  waiting for transfers between devices  10 us (3%)
  starting transfers between devices  9.28 us (3%)
    psum x1, blocking collectives, local_step(): return lax.psum(y_part, 'tp').astype(jnp.bfloat16)  182 us
    dot_general x1, matrix products, local_step(): jnp.einsum('htv,hvd->td', attn_out, w_o.reshape(heads_loc, value_dim, -1)...  21.7 us
    dot_general x4, matrix products, block_stats(): jnp.einsum('hqk,khv->hqv', prob_tile.astype(jnp.bfloat16), v_rows, prefer...  12 us
    dot_general x4, matrix products, up_project(): jnp.dot(lat_rows, w_uk, preferred_element_type=jnp.float32)  11.7 us
    ppermute x3, waiting for transfers between devices, ctx_step(): rot_blk = lax.ppermute(rot_blk, 'ctx', next_perm)  10 us
    ppermute x3, starting transfers between devices, ctx_step(): rot_blk = lax.ppermute(rot_blk, 'ctx', next_perm)  8.02 us
    dot_general x1, matrix products, project_tokens(): jnp.dot(tok_x, w_dq, preferred_element_type=jnp.float32)  7.8 us
    dot_general x4, matrix products, block_scores(): jnp.einsum('qhn,khn->hqk', q_nope, k_nope, preferred_element_type=jnp.flo...  7.37 us
  transfers between devices with their start and end apart: 6, of which 3 were waited for; matrix products, arithmetic and copies ran while one was open for 0% of the time, Pallas kernels for 0%

commit v1 on v0

--- a/solution.py
+++ b/solution.py
@@ -1,6 +1,8 @@
 import jax
 import jax.numpy as jnp
 from jax import lax
+from jax.experimental import pallas as pl
+from jax.experimental.pallas import tpu as pltpu
 from jax.sharding import PartitionSpec as P
 
 ROPE_BASE = 10000.0
@@ -68,6 +70,172 @@
     old_w = jnp.exp(old_max - top_max)
     new_w = jnp.exp(new_max - top_max)
     return top_max, old_sum * old_w + new_sum * new_w, old_acc * old_w[..., None] + new_acc * new_w[..., None]
+
+
+TP = 4
+ROW_BLK = 128
+COL_BLK = 256
+SLOTS = 3
+FIRST_EVENT = 3
+
+
+def out_sum_kernel(o_ref, w_hbm, y_ref, acc, rbuf, wbuf, w_sem, f_send, f_recv, b_send, b_recv):
+    my_tp = lax.axis_index('tp')
+    n_rows, n_cols = y_ref.shape
+    row_blks = n_rows // ROW_BLK
+    half_cols = n_cols // 2
+    col_steps = half_cols // COL_BLK
+    n_chunks = col_steps * row_blks
+    left = lax.rem(my_tp + TP - 1, TP)
+    right = lax.rem(my_tp + 1, TP)
+    depth = (TP - 1 - my_tp, my_tp)
+    onward = (left, right)
+    back = (right, left)
+
+    def w_copy(step, side):
+        slot = lax.rem(step, SLOTS)
+        cols = pl.ds(pl.multiple_of(side * half_cols + step * COL_BLK, COL_BLK), COL_BLK)
+        return pltpu.make_async_copy(w_hbm.at[:, cols], wbuf.at[slot, side], w_sem.at[slot, side])
+
+    def y_slice(side, chunk):
+        step, row = chunk // row_blks, lax.rem(chunk, row_blks)
+        return (pl.ds(pl.multiple_of(row * ROW_BLK, ROW_BLK), ROW_BLK),
+                pl.ds(pl.multiple_of(side * half_cols + step * COL_BLK, COL_BLK), COL_BLK))
+
+    def f_copy(side, chunk):
+        return pltpu.make_async_remote_copy(
+            src_ref=acc.at[side, chunk], dst_ref=rbuf.at[side, chunk],
+            send_sem=f_send.at[side, chunk], recv_sem=f_recv.at[side, chunk],
+            device_id={'tp': onward[side]}, device_id_type=pl.DeviceIdType.MESH)
+
+    def b_copy(side, chunk):
+        part = y_ref.at[y_slice(side, chunk)]
+        return pltpu.make_async_remote_copy(
+            src_ref=part, dst_ref=part,
+            send_sem=b_send.at[side, chunk], recv_sem=b_recv.at[side, chunk],
+            device_id={'tp': back[side]}, device_id_type=pl.DeviceIdType.MESH)
+
+    for pre in range(SLOTS - 1):
+        for side in range(2):
+            w_copy(pre, side).start()
+
+    barrier = pltpu.get_barrier_semaphore()
+
+    @pl.when(my_tp > 0)
+    def _():
+        pl.semaphore_signal(barrier, inc=1, device_id={'tp': left}, device_id_type=pl.DeviceIdType.MESH)
+
+    @pl.when(my_tp < TP - 1)
+    def _():
+        pl.semaphore_signal(barrier, inc=1, device_id={'tp': right}, device_id_type=pl.DeviceIdType.MESH)
+
+    @pl.when((my_tp > 0) & (my_tp < TP - 1))
+    def _():
+        pl.semaphore_wait(barrier, 2)
+
+    @pl.when((my_tp == 0) | (my_tp == TP - 1))
+    def _():
+        pl.semaphore_wait(barrier, 1)
+
+    def reduce_event(side, chunk):
+        @pl.when(depth[side] > 0)
+        def _():
+            f_copy(side, chunk).wait_recv()
+
+        @pl.when((depth[side] > 0) & (depth[side] < TP - 1))
+        def _():
+            acc[side, chunk] = acc[side, chunk] + rbuf[side, chunk]
+            f_copy(side, chunk).start()
+
+        @pl.when(depth[side] == TP - 1)
+        def _():
+            total = acc[side, chunk] + rbuf[side, chunk]
+            y_ref[y_slice(side, chunk)] = total.astype(y_ref.dtype)
+            b_copy(side, chunk).start()
+
+    def compute_step(step, _):
+        slot = lax.rem(step, SLOTS)
+
+        @pl.when(step + SLOTS - 1 < col_steps)
+        def _():
+            for side in range(2):
+                w_copy(step + SLOTS - 1, side).start()
+
+        for side in range(2):
+            w_copy(step, side).wait()
+            part = jnp.dot(o_ref[...], wbuf[slot, side], preferred_element_type=jnp.float32)
+            for row in range(row_blks):
+                chunk = step * row_blks + row
+                acc[side, chunk] = part[row * ROW_BLK:(row + 1) * ROW_BLK]
+
+                @pl.when(depth[side] == 0)
+                def _():
+                    f_copy(side, chunk).start()
+
+        @pl.when(step >= FIRST_EVENT)
+        def _():
+            for side in range(2):
+                reduce_event(side, step - FIRST_EVENT)
+        return 0
+
+    lax.fori_loop(0, col_steps, compute_step, 0)
+
+    def late_event(chunk, _):
+        for side in range(2):
+            reduce_event(side, chunk)
+        return 0
+
+    lax.fori_loop(col_steps - FIRST_EVENT, n_chunks, late_event, 0)
+
+    def back_event(chunk, _):
+        for side in range(2):
+            @pl.when(depth[side] < TP - 1)
+            def _():
+                b_copy(side, chunk).wait_recv()
+
+            @pl.when((depth[side] > 0) & (depth[side] < TP - 1))
+            def _():
+                b_copy(side, chunk).start()
+        return 0
+
+    lax.fori_loop(0, n_chunks, back_event, 0)
+
+    def drain(chunk, _):
+        for side in range(2):
+            @pl.when(depth[side] < TP - 1)
+            def _():
+                f_copy(side, chunk).wait_send()
+
+            @pl.when(depth[side] > 0)
+            def _():
+                b_copy(side, chunk).wait_send()
+        return 0
+
+    lax.fori_loop(0, n_chunks, drain, 0)
+
+
+def out_sum(attn_out, w_o):
+    n_rows, n_depth = attn_out.shape
+    n_cols = w_o.shape[1]
+    n_chunks = (n_cols // 2 // COL_BLK) * (n_rows // ROW_BLK)
+    return pl.pallas_call(
+        out_sum_kernel,
+        out_shape=jax.ShapeDtypeStruct((n_rows, n_cols), jnp.bfloat16),
+        in_specs=[pl.BlockSpec(memory_space=pltpu.VMEM), pl.BlockSpec(memory_space=pl.ANY)],
+        out_specs=pl.BlockSpec(memory_space=pltpu.VMEM),
+        scratch_shapes=[
+            pltpu.VMEM((2, n_chunks, ROW_BLK, COL_BLK), jnp.float32),
+            pltpu.VMEM((2, n_chunks, ROW_BLK, COL_BLK), jnp.float32),
+            pltpu.VMEM((SLOTS, 2, n_depth, COL_BLK), jnp.bfloat16),
+            pltpu.SemaphoreType.DMA((SLOTS, 2)),
+            pltpu.SemaphoreType.DMA((2, n_chunks)),
+            pltpu.SemaphoreType.DMA((2, n_chunks)),
+            pltpu.SemaphoreType.DMA((2, n_chunks)),
+            pltpu.SemaphoreType.DMA((2, n_chunks)),
+        ],
+        compiler_params=pltpu.CompilerParams(collective_id=0, has_side_effects=True, vmem_limit_bytes=50 * 2 ** 20),
+        name='out_sum',
+    )(attn_out, w_o)
 
 
 def solution(mesh):
@@ -119,8 +287,8 @@
         loop_carry = lax.fori_loop(1, ctx_count, ctx_step, (c_kv, k_pe, run_state))
         run_max, run_sum, run_acc = loop_carry[2]
         attn_out = (run_acc / run_sum[..., None]).astype(jnp.bfloat16)
-        y_part = jnp.einsum('htv,hvd->td', attn_out, w_o.reshape(heads_loc, value_dim, -1), preferred_element_type=jnp.float32)
-        return lax.psum(y_part, 'tp').astype(jnp.bfloat16)
+        attn_rows = attn_out.transpose(1, 0, 2).reshape(tok_x.shape[0], heads_loc * value_dim)
+        return out_sum(attn_rows, w_o)
 
     return jax.shard_map(local_step, mesh=mesh,
                          in_specs=(tok_spec, pos_spec, full_mat, full_vec, col_spec, col_spec, full_mat, full_vec, full_mat, col_spec, col_spec, row_spec),

time: 313 us -> 449 us (1.43)
  Pallas kernels: 0 us -> 332 us
  blocking collectives: 182 us -> 0 us
  matrix products: 85.4 us -> 61.5 us
    pallas_call x0 -> x1, Pallas kernels: none -> 332 us  [out_sum(): pl.pallas_call(out_sum_kernel, out_shape=jax.ShapeDtypeStruct((n_rows, n_...]
    psum x1 -> x0, blocking collectives: 182 us -> none  [local_step(): return lax.psum(y_part, 'tp').astype(jnp.bfloat16)]
    dot_general x1 -> x0, matrix products: 21.7 us -> none  [local_step(): jnp.einsum('htv,hvd->td', attn_out, w_o.reshape(heads_loc, value_dim, -1)...]
where the time goes in v1:
time: 449 us; the launch traced here: 445 us
  Pallas kernels  332 us (74%)
  matrix products  61.5 us (14%)
  other arithmetic  16 us (4%)
  local copies, waits for them, and re-layouts  15.6 us (3%)
  waiting for transfers between devices  10.2 us (2%)
  starting transfers between devices  9.03 us (2%)
    pallas_call x1, Pallas kernels, out_sum(): pl.pallas_call(out_sum_kernel, out_shape=jax.ShapeDtypeStruct((n_rows, n_...  332 us
    dot_general x4, matrix products, block_stats(): jnp.einsum('hqk,khv->hqv', prob_tile.astype(jnp.bfloat16), v_rows, prefer...  11.9 us
    dot_general x4, matrix products, up_project(): jnp.dot(lat_rows, w_uk, preferred_element_type=jnp.float32)  11.7 us
    ppermute x3, waiting for transfers between devices, ctx_step(): rot_blk = lax.ppermute(rot_blk, 'ctx', next_perm)  10.2 us
  transfers between devices with their start and end apart: 6, of which 3 were waited for; matrix products, arithmetic and copies ran while one was open for 0% of the time, Pallas kernels for 0%

profile of v1, /device:TPU:0, one launch (start us, length us, event | category | flops | bytes accessed | tf_op | source)
XLA Modules:
  0.0 445.0 jit_solution(13247073062811631719)
XLA Ops:
  1.7 8.5 %multiply_reduce_fusion = (f32[256]{0:T(256)S(1)}, f32[256,1536]{1,0:T(8,128)S(1)}) fusion(bf16[256,5120]{1,0:T(8,128)(2,1)S(1)} %copy-done, bf16[5120,1536]{1,0:T(8,128)(2,1)} %param.18), kind=kOutput, calls=%fused_computation.74 | convolution fusion | flops 4027318016 | bytes 19923968 | tf_op jit(solution)/shard_map/dot_general | solution.py:36
  10.4 2.8 fusion.53
  15.2 4.1 fusion.49
  27.7 3.7 fusion.40
  36.1 70.5 %while.23 = (s32[]{:T(128)}, bf16[256,512]{1,0:T(8,128)(2,1)S(1)}, bf16[256,64]{0,1:T(8,128)(2,1)S(1)}, f32[32,256]{1,0:T(8,128)S(1)}, f32[32,256]{1,0:T(8,128)S...) while((s32[]{:T(128)}, bf16[256,512]{1,0:T(8,128)(2,1)S(1)}, ...), condition=%wide.region_11.12_spmd, body=%wide.region_4.11_spmd.sunk | while | flops 2830663680 | bytes 97927776 | solution.py:287
  36.6 2.6 collective-permute-start.1
  39.2 3.7 collective-permute-done.1
  42.9 17.0 %conditional.2 = (f32[32,256]{1,0:T(8,128)S(1)}, f32[32,256]{1,0:T(8,128)S(1)}, f32[32,256,128]{2,1,0:T(8,128)}) conditional(s32[]{:T(128)} %convert_element_type.108, (f32[32,256]{1,0:T(8,128)S(1)}, bf16[256,512]{1,0:T(8,128)(2,1)S(1)}, bf16[512,4096]{1,0:T(8,128)(2,1)}, bf16[256,32,128]{2,0,1:T(8,128)(2,1)}, bf16[256,32,64]{0,2,1:T(8,128)(2,1)}, ...), branch_computations={%region_5.7_spmd, %region_8.10_spmd} | conditional | flops 2830663680 | bytes 96157808 | solution.py:284
  42.9 3.5 fusion.10
  54.6 2.7 multiply_add_fusion
  57.5 2.4 pad_maximum_fusion
  60.3 2.5 collective-permute-start.1
  62.8 3.4 collective-permute-done.1
  66.2 17.0 %conditional.2 = (f32[32,256]{1,0:T(8,128)S(1)}, f32[32,256]{1,0:T(8,128)S(1)}, f32[32,256,128]{2,1,0:T(8,128)}) conditional(s32[]{:T(128)} %convert_element_type.108, (f32[32,256]{1,0:T(8,128)S(1)}, bf16[256,512]{1,0:T(8,128)(2,1)S(1)}, bf16[512,4096]{1,0:T(8,128)(2,1)}, bf16[256,32,128]{2,0,1:T(8,128)(2,1)}, bf16[256,32,64]{0,2,1:T(8,128)(2,1)}, ...), branch_computations={%region_5.7_spmd, %region_8.10_spmd} | conditional | flops 2830663680 | bytes 96157808 | solution.py:284
  66.2 3.5 fusion.10
  77.8 2.7 multiply_add_fusion
  83.6 2.8 collective-permute-start.1
  86.4 3.1 collective-permute-done.1
  89.5 17.0 %conditional.2 = (f32[32,256]{1,0:T(8,128)S(1)}, f32[32,256]{1,0:T(8,128)S(1)}, f32[32,256,128]{2,1,0:T(8,128)}) conditional(s32[]{:T(128)} %convert_element_type.108, (f32[32,256]{1,0:T(8,128)S(1)}, bf16[256,512]{1,0:T(8,128)(2,1)S(1)}, bf16[512,4096]{1,0:T(8,128)(2,1)}, bf16[256,32,128]{2,0,1:T(8,128)(2,1)}, bf16[256,32,64]{0,2,1:T(8,128)(2,1)}, ...), branch_computations={%region_5.7_spmd, %region_8.10_spmd} | conditional | flops 2830663680 | bytes 96157808 | solution.py:284
  89.5 3.5 fusion.10
  101.1 2.7 multiply_add_fusion
  106.6 2.9 copy_bitcast_fusion.o_ref
  109.5 332.1 %out_sum.1 = bf16[256,5120]{1,0:T(8,128)(2,1)} custom-call(bf16[256,4096]{1,0:T(8,128)(2,1)S(1)} %copy_bitcast_fusion.o_ref, bf16[4096,5120]{1,0:T(8,128)(2,1)} %w_hbm.1), custom_call_target="tpu_custom_call" | custom-call | tf_op jit(solution)/shard_map/out_sum/pallas_call | solution.py:221
  441.6 3.4 copy.111
  (92 shorter events, 47.7 us)
Async XLA Ops:
  0.0 1.7 copy-start
  0.0 10.3 %copy-start.11 = (bf16[1536]{0:T(1024)(128)(2,1)S(1)}, bf16[1536]{0:T(1024)(128)(2,1)}, u32[]{:S(2)}) copy-start(bf16[1536]{0:T(1024)(128)(2,1)} %param.19) | copy-start | bytes 9220
  0.0 10.3 %copy-start.14 = (bf16[1536,2048]{1,0:T(8,128)(2,1)S(1)}, bf16[1536,2048]{1,0:T(8,128)(2,1)}, u32[]{:S(2)}) copy-start(bf16[1536,2048]{1,0:T(8,128)(2,1)} %param.21) | copy-start | bytes 18874372
  10.3 2.9 copy-start.9
  10.4 3.8 copy-start.10
  10.4 4.8 %copy-start.13 = (bf16[1536,4096]{1,0:T(8,128)(2,1)S(1)}, bf16[1536,4096]{1,0:T(8,128)(2,1)}, u32[]{:S(2)}) copy-start(bf16[1536,4096]{1,0:T(8,128)(2,1)} %param.20) | copy-start | bytes 37748740
  14.4 4.9 %slice-start = ((s8[5242880]{0:T(1024)(128)(4,1)}), s8[4194304]{0:T(1024)(128)(4,1)S(1)}, s32[]{:S(2)}) async-start(s8[5242880]{0:T(1024)(128)(4,1)} %bitcast.99), calls=%async_computation | async-start | bytes 8388608
  15.2 4.1 slice-start.1
  19.3 1.7 copy-start.12
  19.3 2.2 copy-start.5
  24.2 2.2 copy-start.6
  36.1 6.9 %collective-permute-start = (bf16[256,512]{1,0:T(8,128)(2,1)S(1)}, bf16[256,512]{1,0:T(8,128)(2,1)S(1)}, u32[]{:S(2)}, u32[]{:S(2)}) collective-permute-start(bf16[256,512]{1,0:T(8,128)(2,1)S(1)} %get-tuple-element.514), channel_id=1, source_target_pairs={{0,1},{1,2},{2,3},{3,0},{4,5},{5,6},{6,7},{7,4},{8,9},{9,10},{10,1... | collective-permute-start | bytes 786440 | tf_op jit(solution)/shard_map/while/body/eval_jaxpr/ppermute | solution.py:281
  36.6 6.3 %collective-permute-start.1 = (bf16[256,64]{0,1:T(8,128)(2,1)S(1)}, bf16[256,64]{0,1:T(8,128)(2,1)S(1)}, u32[]{:S(2)}, u32[]{:S(2)}) collective-permute-start(bf16[256,64]{0,1:T(8,128)(2,1)S(1)} %get-tuple-element.515), channel_id=1, source_target_pairs={{0,1},{1,2},{2,3},{3,0},{4,5},{5,6},{6,7},{7,4},{8,9},{9,10},{10,1... | collective-permute-start | bytes 98312 | tf_op jit(solution)/shard_map/while/body/eval_jaxpr/ppermute | solution.py:282
  50.2 2.2 copy-start.7
  52.4 2.2 copy-start.2
  60.0 6.2 %collective-permute-start = (bf16[256,512]{1,0:T(8,128)(2,1)S(1)}, bf16[256,512]{1,0:T(8,128)(2,1)S(1)}, u32[]{:S(2)}, u32[]{:S(2)}) collective-permute-start(bf16[256,512]{1,0:T(8,128)(2,1)S(1)} %get-tuple-element.514), channel_id=1, source_target_pairs={{0,1},{1,2},{2,3},{3,0},{4,5},{5,6},{6,7},{7,4},{8,9},{9,10},{10,1... | collective-permute-start | bytes 786440 | tf_op jit(solution)/shard_map/while/body/eval_jaxpr/ppermute | solution.py:281
  60.3 5.9 %collective-permute-start.1 = (bf16[256,64]{0,1:T(8,128)(2,1)S(1)}, bf16[256,64]{0,1:T(8,128)(2,1)S(1)}, u32[]{:S(2)}, u32[]{:S(2)}) collective-permute-start(bf16[256,64]{0,1:T(8,128)(2,1)S(1)} %get-tuple-element.515), channel_id=1, source_target_pairs={{0,1},{1,2},{2,3},{3,0},{4,5},{5,6},{6,7},{7,4},{8,9},{9,10},{10,1... | collective-permute-start | bytes 98312 | tf_op jit(solution)/shard_map/while/body/eval_jaxpr/ppermute | solution.py:282
  73.5 2.2 copy-start.7
  75.7 2.2 copy-start.2
  83.3 6.2 %collective-permute-start = (bf16[256,512]{1,0:T(8,128)(2,1)S(1)}, bf16[256,512]{1,0:T(8,128)(2,1)S(1)}, u32[]{:S(2)}, u32[]{:S(2)}) collective-permute-start(bf16[256,512]{1,0:T(8,128)(2,1)S(1)} %get-tuple-element.514), channel_id=1, source_target_pairs={{0,1},{1,2},{2,3},{3,0},{4,5},{5,6},{6,7},{7,4},{8,9},{9,10},{10,1... | collective-permute-start | bytes 786440 | tf_op jit(solution)/shard_map/while/body/eval_jaxpr/ppermute | solution.py:281
  83.6 5.9 %collective-permute-start.1 = (bf16[256,64]{0,1:T(8,128)(2,1)S(1)}, bf16[256,64]{0,1:T(8,128)(2,1)S(1)}, u32[]{:S(2)}, u32[]{:S(2)}) collective-permute-start(bf16[256,64]{0,1:T(8,128)(2,1)S(1)} %get-tuple-element.515), channel_id=1, source_target_pairs={{0,1},{1,2},{2,3},{3,0},{4,5},{5,6},{6,7},{7,4},{8,9},{9,10},{10,1... | collective-permute-start | bytes 98312 | tf_op jit(solution)/shard_map/while/body/eval_jaxpr/ppermute | solution.py:282
  96.8 2.2 copy-start.7
  98.9 2.2 copy-start.2
  109.5 335.5 %copy-start.1 = (bf16[256,5120]{1,0:T(8,128)(2,1)S(1)}, bf16[256,5120]{1,0:T(8,128)(2,1)}, u32[]{:S(2)}) copy-start(bf16[256,5120]{1,0:T(8,128)(2,1)} %param.16) | copy-start | bytes 7864324

commit v2 on v1

--- a/solution.py
+++ b/solution.py
@@ -77,6 +77,8 @@
 COL_BLK = 256
 SLOTS = 3
 FIRST_EVENT = 3
+SUM_LAG = 2
+BACK_LAG = 3
 
 
 def out_sum_kernel(o_ref, w_hbm, y_ref, acc, rbuf, wbuf, w_sem, f_send, f_recv, b_send, b_recv):
@@ -137,17 +139,20 @@
     def _():
         pl.semaphore_wait(barrier, 1)
 
-    def reduce_event(side, chunk):
-        @pl.when(depth[side] > 0)
+    def reduce_event(side, event):
+        chunk = event - SUM_LAG * (depth[side] - 1)
+        live = (chunk >= 0) & (chunk < n_chunks)
+
+        @pl.when(live & (depth[side] > 0))
         def _():
             f_copy(side, chunk).wait_recv()
 
-        @pl.when((depth[side] > 0) & (depth[side] < TP - 1))
+        @pl.when(live & (depth[side] > 0) & (depth[side] < TP - 1))
         def _():
             acc[side, chunk] = acc[side, chunk] + rbuf[side, chunk]
             f_copy(side, chunk).start()
 
-        @pl.when(depth[side] == TP - 1)
+        @pl.when(live & (depth[side] == TP - 1))
         def _():
             total = acc[side, chunk] + rbuf[side, chunk]
             y_ref[y_slice(side, chunk)] = total.astype(y_ref.dtype)
@@ -180,25 +185,28 @@
 
     lax.fori_loop(0, col_steps, compute_step, 0)
 
-    def late_event(chunk, _):
-        for side in range(2):
-            reduce_event(side, chunk)
+    def late_event(event, _):
+        for side in range(2):
+            reduce_event(side, event)
         return 0
 
-    lax.fori_loop(col_steps - FIRST_EVENT, n_chunks, late_event, 0)
-
-    def back_event(chunk, _):
-        for side in range(2):
-            @pl.when(depth[side] < TP - 1)
+    lax.fori_loop(col_steps - FIRST_EVENT, n_chunks + SUM_LAG * (TP - 2), late_event, 0)
+
+    def back_event(event, _):
+        for side in range(2):
+            chunk = event - BACK_LAG * (TP - 2 - depth[side])
+            live = (chunk >= 0) & (chunk < n_chunks)
+
+            @pl.when(live & (depth[side] < TP - 1))
             def _():
                 b_copy(side, chunk).wait_recv()
 
-            @pl.when((depth[side] > 0) & (depth[side] < TP - 1))
+            @pl.when(live & (depth[side] > 0) & (depth[side] < TP - 1))
             def _():
                 b_copy(side, chunk).start()
         return 0
 
-    lax.fori_loop(0, n_chunks, back_event, 0)
+    lax.fori_loop(0, n_chunks + BACK_LAG * (TP - 2), back_event, 0)
 
     def drain(chunk, _):
         for side in range(2):

time: 449 us -> 221 us (0.49)
  Pallas kernels: 332 us -> 108 us
    pallas_call x1, Pallas kernels: 332 us -> 108 us  [out_sum(): pl.pallas_call(out_sum_kernel, out_shape=jax.ShapeDtypeStruct((n_rows, n_...]
where the time goes in v2:
time: 221 us; the launch traced here: 220 us
  Pallas kernels  108 us (49%)
  matrix products  61.5 us (28%)
  other arithmetic  16 us (7%)
  local copies, waits for them, and re-layouts  15.6 us (7%)
  waiting for transfers between devices  10.2 us (5%)
  starting transfers between devices  9.03 us (4%)
    pallas_call x1, Pallas kernels, out_sum(): pl.pallas_call(out_sum_kernel, out_shape=jax.ShapeDtypeStruct((n_rows, n_...  108 us
    dot_general x4, matrix products, block_stats(): jnp.einsum('hqk,khv->hqv', prob_tile.astype(jnp.bfloat16), v_rows, prefer...  11.9 us
    dot_general x4, matrix products, up_project(): jnp.dot(lat_rows, w_uk, preferred_element_type=jnp.float32)  11.7 us
    ppermute x3, waiting for transfers between devices, ctx_step(): rot_blk = lax.ppermute(rot_blk, 'ctx', next_perm)  10.2 us
    dot_general x1, matrix products, project_tokens(): jnp.dot(tok_x, w_dq, preferred_element_type=jnp.float32)  8.55 us
    ppermute x3, starting transfers between devices, ctx_step(): rot_blk = lax.ppermute(rot_blk, 'ctx', next_perm)  7.93 us
    dot_general x4, matrix products, block_scores(): jnp.einsum('qhn,khn->hqk', q_nope, k_nope, preferred_element_type=jnp.flo...  7.37 us
    concatenate x3, other arithmetic, attend_upper(): jnp.concatenate([old_acc[:, :half_len], top_acc], axis=1)  7.27 us
  transfers between devices with their start and end apart: 6, of which 3 were waited for; matrix products, arithmetic and copies ran while one was open for 0% of the time, Pallas kernels for 0%

profile of v2, /device:TPU:0, one launch (start us, length us, event | category | flops | bytes accessed | tf_op | source)
XLA Modules:
  0.0 220.5 jit_solution(11074116872302115562)
XLA Ops:
  1.7 8.5 %multiply_reduce_fusion = (f32[256]{0:T(256)S(1)}, f32[256,1536]{1,0:T(8,128)S(1)}) fusion(bf16[256,5120]{1,0:T(8,128)(2,1)S(1)} %copy-done, bf16[5120,1536]{1,0:T(8,128)(2,1)} %param.18), kind=kOutput, calls=%fused_computation.74 | convolution fusion | flops 4027318016 | bytes 19923968 | tf_op jit(solution)/shard_map/dot_general | solution.py:36
  10.4 2.8 %fusion.53 = f32[256,2048]{0,1:T(8,128)S(1)} fusion(bf16[1536,2048]{1,0:T(8,128)(2,1)S(1)} %copy-done.14, f32[256,1536]{1,0:T(8,128)S(1)} %get-tuple-element.416, f32[1536]{0:T(1024)S(1)} %convert_element_type.63, f32[256]{0:T(256)S(1)} %add_rsqrt_fusion), kind=kOutput, calls=%fused_computation.90 | convolution fusion | flops 1611792384 | bytes 9968640 | tf_op jit(solution)/shard_map/dot_general | solution.py:38
  15.2 4.1 %fusion.49 = bf16[32,32,8,128]{3,2,1,0:T(8,128)(2,1)S(1)} fusion(bf16[1536,4096]{1,0:T(8,128)(2,1)S(1)} %copy-done.13, f32[256,1536]{1,0:T(8,128)S(1)} %get-tuple-element.416, f32[1536]{0:T(1024)S(1)} %convert_element_type.63, f32[256]{0:T(256)S(1)} %add_rsqrt_fusion), kind=kOutput, calls=%fused_computation.70 | convolution fusion | flops 3223453696 | bytes 16260096 | tf_op jit(solution)/shard_map/dot_general | solution.py:37
  27.7 3.7 %fusion.40 = f32[32,256,128]{2,1,0:T(8,128)} fusion(f32[32,256,256]{1,2,0:T(8,128)S(1)} %get-tuple-element.418, f32[32,256]{1,0:T(8,128)S(1)} %get-tuple-element.501, bf16[32,32,8,128]{3,2,1,0:T(8,128)(2,1)S(1)} %fusion.51), kind=kOutput, calls=%fused_computation.59 | convolution fusion | flops 541065216 | bytes 14712832 | tf_op jit(solution)/shard_map/hqk,khv->hqv/dot_general | solution.py:62
  36.1 70.5 %while.23 = (s32[]{:T(128)}, bf16[256,512]{1,0:T(8,128)(2,1)S(1)}, bf16[256,64]{0,1:T(8,128)(2,1)S(1)}, f32[32,256]{1,0:T(8,128)S(1)}, f32[32,256]{1,0:T(8,128)S...) while((s32[]{:T(128)}, bf16[256,512]{1,0:T(8,128)(2,1)S(1)}, ...), condition=%wide.region_11.12_spmd, body=%wide.region_4.11_spmd.sunk | while | flops 2830663680 | bytes 97927776 | solution.py:295
  36.6 2.6 %collective-permute-start.1 = (bf16[256,64]{0,1:T(8,128)(2,1)S(1)}, bf16[256,64]{0,1:T(8,128)(2,1)S(1)}, u32[]{:S(2)}, u32[]{:S(2)}) collective-permute-start(bf16[256,64]{0,1:T(8,128)(2,1)S(1)} %get-tuple-element.515), channel_id=1, source_target_pairs={{0,1},{1,2},{2,3},{3,0},{4,5},{5,6},{6,7},{7,4},{8,9},{9,10},{10,1... | collective-permute-start | bytes 98312 | tf_op jit(solution)/shard_map/while/body/eval_jaxpr/ppermute | solution.py:290
  39.2 3.7 %collective-permute-done.1 = bf16[256,64]{0,1:T(8,128)(2,1)S(1)} collective-permute-done((bf16[256,64]{0,1:T(8,128)(2,1)S(1)}, bf16[256,64]{0,1:T(8,128)(2,1)S(1)}, u32[]{:S(2)}, u32[]{:S(2)}) %collective-permute-start.1) | collective-permute-done | bytes 32800 | tf_op jit(solution)/shard_map/while/body/eval_jaxpr/ppermute | solution.py:290
  42.9 17.0 %conditional.2 = (f32[32,256]{1,0:T(8,128)S(1)}, f32[32,256]{1,0:T(8,128)S(1)}, f32[32,256,128]{2,1,0:T(8,128)}) conditional(s32[]{:T(128)} %convert_element_type.108, (f32[32,256]{1,0:T(8,128)S(1)}, bf16[256,512]{1,0:T(8,128)(2,1)S(1)}, bf16[512,4096]{1,0:T(8,128)(2,1)}, bf16[256,32,128]{2,0,1:T(8,128)(2,1)}, bf16[256,32,64]{0,2,1:T(8,128)(2,1)}, ...), branch_computations={%region_5.7_spmd, %region_8.10_spmd} | conditional | flops 2830663680 | bytes 96157808 | solution.py:292
  42.9 3.5 %fusion.10 = bf16[32,32,8,128]{3,2,1,0:T(8,128)(2,1)S(1)} fusion(bf16[256,512]{1,0:T(8,128)(2,1)S(1)} %get-tuple-element.309, bf16[512,4096]{1,0:T(8,128)(2,1)} %get-tuple-element.310), kind=kOutput, calls=%fused_computation.15 | convolution fusion | flops 1074790400 | bytes 6553600 | tf_op jit(solution)/shard_map/while/body/eval_jaxpr/cond/branch_0_fun/dot_general | solution.py:47
  54.6 2.7 %multiply_add_fusion = f32[32,128,128]{2,1,0:T(8,128)S(1)} fusion(f32[32,256,128]{2,1,0:T(8,128)S(1)} %copy-done.2, bf16[32,32,8,128]{3,2,1,0:T(8,128)(2,1)S(1)} %fusion.11, f32[32,128,256]{1,2,0:T(8,128)S(1)} %get-tuple-element.400, f32[32,128]{1,0:T(8,128)S(1)} %get-tuple-element.399, f32[32,128]{1,0:T(8,128)S(1)} %get-tuple-element.391, ...), kind=kOutput, calls=%fused_computation.13 | convolution fusion | flops 272105472 | bytes 10534912 | tf_op jit(solution)/shard_map/while/body/eval_jaxpr/cond/branch_0_fun/hqk,khv->hqv/dot_general | solution.py:62
  57.5 2.4 %pad_maximum_fusion = f32[32,256,128]{2,1,0:T(8,128)} fusion(f32[32,128,128]{2,1,0:T(8,128)S(1)} %multiply_add_fusion, f32[32,128,128]{2,1,0:T(8,128)S(1)} %slice.34), kind=kLoop, calls=%fused_computation.2 | loop fusion | flops 1048576 | bytes 8388608 | tf_op jit(solution)/shard_map/while/body/eval_jaxpr/cond/branch_0_fun/concatenate | solution.py:285
  60.3 2.5 %collective-permute-start.1 = (bf16[256,64]{0,1:T(8,128)(2,1)S(1)}, bf16[256,64]{0,1:T(8,128)(2,1)S(1)}, u32[]{:S(2)}, u32[]{:S(2)}) collective-permute-start(bf16[256,64]{0,1:T(8,128)(2,1)S(1)} %get-tuple-element.515), channel_id=1, source_target_pairs={{0,1},{1,2},{2,3},{3,0},{4,5},{5,6},{6,7},{7,4},{8,9},{9,10},{10,1... | collective-permute-start | bytes 98312 | tf_op jit(solution)/shard_map/while/body/eval_jaxpr/ppermute | solution.py:290
  62.8 3.4 %collective-permute-done.1 = bf16[256,64]{0,1:T(8,128)(2,1)S(1)} collective-permute-done((bf16[256,64]{0,1:T(8,128)(2,1)S(1)}, bf16[256,64]{0,1:T(8,128)(2,1)S(1)}, u32[]{:S(2)}, u32[]{:S(2)}) %collective-permute-start.1) | collective-permute-done | bytes 32800 | tf_op jit(solution)/shard_map/while/body/eval_jaxpr/ppermute | solution.py:290
  66.2 17.0 %conditional.2 = (f32[32,256]{1,0:T(8,128)S(1)}, f32[32,256]{1,0:T(8,128)S(1)}, f32[32,256,128]{2,1,0:T(8,128)}) conditional(s32[]{:T(128)} %convert_element_type.108, (f32[32,256]{1,0:T(8,128)S(1)}, bf16[256,512]{1,0:T(8,128)(2,1)S(1)}, bf16[512,4096]{1,0:T(8,128)(2,1)}, bf16[256,32,128]{2,0,1:T(8,128)(2,1)}, bf16[256,32,64]{0,2,1:T(8,128)(2,1)}, ...), branch_computations={%region_5.7_spmd, %region_8.10_spmd} | conditional | flops 2830663680 | bytes 96157808 | solution.py:292
  66.2 3.5 %fusion.10 = bf16[32,32,8,128]{3,2,1,0:T(8,128)(2,1)S(1)} fusion(bf16[256,512]{1,0:T(8,128)(2,1)S(1)} %get-tuple-element.309, bf16[512,4096]{1,0:T(8,128)(2,1)} %get-tuple-element.310), kind=kOutput, calls=%fused_computation.15 | convolution fusion | flops 1074790400 | bytes 6553600 | tf_op jit(solution)/shard_map/while/body/eval_jaxpr/cond/branch_0_fun/dot_general | solution.py:47
  77.8 2.7 %multiply_add_fusion = f32[32,128,128]{2,1,0:T(8,128)S(1)} fusion(f32[32,256,128]{2,1,0:T(8,128)S(1)} %copy-done.2, bf16[32,32,8,128]{3,2,1,0:T(8,128)(2,1)S(1)} %fusion.11, f32[32,128,256]{1,2,0:T(8,128)S(1)} %get-tuple-element.400, f32[32,128]{1,0:T(8,128)S(1)} %get-tuple-element.399, f32[32,128]{1,0:T(8,128)S(1)} %get-tuple-element.391, ...), kind=kOutput, calls=%fused_computation.13 | convolution fusion | flops 272105472 | bytes 10534912 | tf_op jit(solution)/shard_map/while/body/eval_jaxpr/cond/branch_0_fun/hqk,khv->hqv/dot_general | solution.py:62
  83.6 2.8 %collective-permute-start.1 = (bf16[256,64]{0,1:T(8,128)(2,1)S(1)}, bf16[256,64]{0,1:T(8,128)(2,1)S(1)}, u32[]{:S(2)}, u32[]{:S(2)}) collective-permute-start(bf16[256,64]{0,1:T(8,128)(2,1)S(1)} %get-tuple-element.515), channel_id=1, source_target_pairs={{0,1},{1,2},{2,3},{3,0},{4,5},{5,6},{6,7},{7,4},{8,9},{9,10},{10,1... | collective-permute-start | bytes 98312 | tf_op jit(solution)/shard_map/while/body/eval_jaxpr/ppermute | solution.py:290
  86.4 3.1 %collective-permute-done.1 = bf16[256,64]{0,1:T(8,128)(2,1)S(1)} collective-permute-done((bf16[256,64]{0,1:T(8,128)(2,1)S(1)}, bf16[256,64]{0,1:T(8,128)(2,1)S(1)}, u32[]{:S(2)}, u32[]{:S(2)}) %collective-permute-start.1) | collective-permute-done | bytes 32800 | tf_op jit(solution)/shard_map/while/body/eval_jaxpr/ppermute | solution.py:290
  89.5 17.0 %conditional.2 = (f32[32,256]{1,0:T(8,128)S(1)}, f32[32,256]{1,0:T(8,128)S(1)}, f32[32,256,128]{2,1,0:T(8,128)}) conditional(s32[]{:T(128)} %convert_element_type.108, (f32[32,256]{1,0:T(8,128)S(1)}, bf16[256,512]{1,0:T(8,128)(2,1)S(1)}, bf16[512,4096]{1,0:T(8,128)(2,1)}, bf16[256,32,128]{2,0,1:T(8,128)(2,1)}, bf16[256,32,64]{0,2,1:T(8,128)(2,1)}, ...), branch_computations={%region_5.7_spmd, %region_8.10_spmd} | conditional | flops 2830663680 | bytes 96157808 | solution.py:292
  89.5 3.5 %fusion.10 = bf16[32,32,8,128]{3,2,1,0:T(8,128)(2,1)S(1)} fusion(bf16[256,512]{1,0:T(8,128)(2,1)S(1)} %get-tuple-element.309, bf16[512,4096]{1,0:T(8,128)(2,1)} %get-tuple-element.310), kind=kOutput, calls=%fused_computation.15 | convolution fusion | flops 1074790400 | bytes 6553600 | tf_op jit(solution)/shard_map/while/body/eval_jaxpr/cond/branch_0_fun/dot_general | solution.py:47
  101.1 2.7 %multiply_add_fusion = f32[32,128,128]{2,1,0:T(8,128)S(1)} fusion(f32[32,256,128]{2,1,0:T(8,128)S(1)} %copy-done.2, bf16[32,32,8,128]{3,2,1,0:T(8,128)(2,1)S(1)} %fusion.11, f32[32,128,256]{1,2,0:T(8,128)S(1)} %get-tuple-element.400, f32[32,128]{1,0:T(8,128)S(1)} %get-tuple-element.399, f32[32,128]{1,0:T(8,128)S(1)} %get-tuple-element.391, ...), kind=kOutput, calls=%fused_computation.13 | convolution fusion | flops 272105472 | bytes 10534912 | tf_op jit(solution)/shard_map/while/body/eval_jaxpr/cond/branch_0_fun/hqk,khv->hqv/dot_general | solution.py:62
  106.6 2.9 %copy_bitcast_fusion.o_ref = bf16[256,4096]{1,0:T(8,128)(2,1)S(1)} fusion(f32[32,256,128]{2,1,0:T(8,128)} %get-tuple-element.343, f32[32,256]{1,0:T(8,128)S(1)} %get-tuple-element.344), kind=kLoop, calls=%fused_computation.62 | loop fusion | flops 2097152 | bytes 6324224 | tf_op jit(solution)/shard_map/reshape | solution.py:298
  109.5 107.6 %out_sum.1 = bf16[256,5120]{1,0:T(8,128)(2,1)} custom-call(bf16[256,4096]{1,0:T(8,128)(2,1)S(1)} %copy_bitcast_fusion.o_ref, bf16[4096,5120]{1,0:T(8,128)(2,1)} %w_hbm.1), custom_call_target="tpu_custom_call" | custom-call | tf_op jit(solution)/shard_map/out_sum/pallas_call | solution.py:229
  217.1 3.4 %copy.111 = bf16[256,5120]{1,0:T(8,128)(2,1)} copy(bf16[256,5120]{1,0:T(8,128)(2,1)} %out_sum.1) | data formatting | bytes 5242880
  (92 shorter events, 47.7 us)
Async XLA Ops:
  0.0 1.7 copy-start
  0.0 10.3 %copy-start.11 = (bf16[1536]{0:T(1024)(128)(2,1)S(1)}, bf16[1536]{0:T(1024)(128)(2,1)}, u32[]{:S(2)}) copy-start(bf16[1536]{0:T(1024)(128)(2,1)} %param.19) | copy-start | bytes 9220
  0.0 10.3 %copy-start.14 = (bf16[1536,2048]{1,0:T(8,128)(2,1)S(1)}, bf16[1536,2048]{1,0:T(8,128)(2,1)}, u32[]{:S(2)}) copy-start(bf16[1536,2048]{1,0:T(8,128)(2,1)} %param.21) | copy-start | bytes 18874372
  10.3 2.9 %copy-start.9 = (bf16[5120,64]{0,1:T(8,128)(2,1)S(1)}, bf16[5120,64]{0,1:T(8,128)(2,1)}, u32[]{:S(2)}) copy-start(bf16[5120,64]{0,1:T(8,128)(2,1)} %param.24) | copy-start | bytes 1966084
  10.4 3.8 %copy-start.10 = (s32[256]{0:T(256)S(1)}, s32[256]{0:T(256)}, u32[]{:S(2)}) copy-start(s32[256]{0:T(256)} %param.17) | copy-start | bytes 3076
  10.4 4.8 %copy-start.13 = (bf16[1536,4096]{1,0:T(8,128)(2,1)S(1)}, bf16[1536,4096]{1,0:T(8,128)(2,1)}, u32[]{:S(2)}) copy-start(bf16[1536,4096]{1,0:T(8,128)(2,1)} %param.20) | copy-start | bytes 37748740
  14.4 4.9 %slice-start = ((s8[5242880]{0:T(1024)(128)(4,1)}), s8[4194304]{0:T(1024)(128)(4,1)S(1)}, s32[]{:S(2)}) async-start(s8[5242880]{0:T(1024)(128)(4,1)} %bitcast.99), calls=%async_computation | async-start | bytes 8388608
  15.2 4.1 %slice-start.1 = ((s8[5242880]{0:T(1024)(128)(4,1)}), s8[1048576]{0:T(1024)(128)(4,1)S(1)}, s32[]{:S(2)}) async-start(s8[5242880]{0:T(1024)(128)(4,1)} %bitcast.99), calls=%async_computation.1 | async-start | bytes 2097152
  19.3 1.7 copy-start.12
  19.3 2.2 copy-start.5
  24.2 2.2 copy-start.6
  36.1 6.9 %collective-permute-start = (bf16[256,512]{1,0:T(8,128)(2,1)S(1)}, bf16[256,512]{1,0:T(8,128)(2,1)S(1)}, u32[]{:S(2)}, u32[]{:S(2)}) collective-permute-start(bf16[256,512]{1,0:T(8,128)(2,1)S(1)} %get-tuple-element.514), channel_id=1, source_target_pairs={{0,1},{1,2},{2,3},{3,0},{4,5},{5,6},{6,7},{7,4},{8,9},{9,10},{10,1... | collective-permute-start | bytes 786440 | tf_op jit(solution)/shard_map/while/body/eval_jaxpr/ppermute | solution.py:289
  36.6 6.3 %collective-permute-start.1 = (bf16[256,64]{0,1:T(8,128)(2,1)S(1)}, bf16[256,64]{0,1:T(8,128)(2,1)S(1)}, u32[]{:S(2)}, u32[]{:S(2)}) collective-permute-start(bf16[256,64]{0,1:T(8,128)(2,1)S(1)} %get-tuple-element.515), channel_id=1, source_target_pairs={{0,1},{1,2},{2,3},{3,0},{4,5},{5,6},{6,7},{7,4},{8,9},{9,10},{10,1... | collective-permute-start | bytes 98312 | tf_op jit(solution)/shard_map/while/body/eval_jaxpr/ppermute | solution.py:290
  50.2 2.2 copy-start.7
  52.4 2.2 copy-start.2
  60.0 6.2 %collective-permute-start = (bf16[256,512]{1,0:T(8,128)(2,1)S(1)}, bf16[256,512]{1,0:T(8,128)(2,1)S(1)}, u32[]{:S(2)}, u32[]{:S(2)}) collective-permute-start(bf16[256,512]{1,0:T(8,128)(2,1)S(1)} %get-tuple-element.514), channel_id=1, source_target_pairs={{0,1},{1,2},{2,3},{3,0},{4,5},{5,6},{6,7},{7,4},{8,9},{9,10},{10,1... | collective-permute-start | bytes 786440 | tf_op jit(solution)/shard_map/while/body/eval_jaxpr/ppermute | solution.py:289
  60.3 5.9 %collective-permute-start.1 = (bf16[256,64]{0,1:T(8,128)(2,1)S(1)}, bf16[256,64]{0,1:T(8,128)(2,1)S(1)}, u32[]{:S(2)}, u32[]{:S(2)}) collective-permute-start(bf16[256,64]{0,1:T(8,128)(2,1)S(1)} %get-tuple-element.515), channel_id=1, source_target_pairs={{0,1},{1,2},{2,3},{3,0},{4,5},{5,6},{6,7},{7,4},{8,9},{9,10},{10,1... | collective-permute-start | bytes 98312 | tf_op jit(solution)/shard_map/while/body/eval_jaxpr/ppermute | solution.py:290
  73.5 2.2 copy-start.7
  75.7 2.2 copy-start.2
  83.3 6.2 %collective-permute-start = (bf16[256,512]{1,0:T(8,128)(2,1)S(1)}, bf16[256,512]{1,0:T(8,128)(2,1)S(1)}, u32[]{:S(2)}, u32[]{:S(2)}) collective-permute-start(bf16[256,512]{1,0:T(8,128)(2,1)S(1)} %get-tuple-element.514), channel_id=1, source_target_pairs={{0,1},{1,2},{2,3},{3,0},{4,5},{5,6},{6,7},{7,4},{8,9},{9,10},{10,1... | collective-permute-start | bytes 786440 | tf_op jit(solution)/shard_map/while/body/eval_jaxpr/ppermute | solution.py:289
  83.6 5.9 %collective-permute-start.1 = (bf16[256,64]{0,1:T(8,128)(2,1)S(1)}, bf16[256,64]{0,1:T(8,128)(2,1)S(1)}, u32[]{:S(2)}, u32[]{:S(2)}) collective-permute-start(bf16[256,64]{0,1:T(8,128)(2,1)S(1)} %get-tuple-element.515), channel_id=1, source_target_pairs={{0,1},{1,2},{2,3},{3,0},{4,5},{5,6},{6,7},{7,4},{8,9},{9,10},{10,1... | collective-permute-start | bytes 98312 | tf_op jit(solution)/shard_map/while/body/eval_jaxpr/ppermute | solution.py:290
  96.8 2.2 copy-start.7
  98.9 2.2 copy-start.2
  109.5 111.0 %copy-start.1 = (bf16[256,5120]{1,0:T(8,128)(2,1)S(1)}, bf16[256,5120]{1,0:T(8,128)(2,1)}, u32[]{:S(2)}) copy-start(bf16[256,5120]{1,0:T(8,128)(2,1)} %param.16) | copy-start | bytes 7864324

commit v3 on v2

v3 whole, which is shorter than its diff:
```python
import math

import jax
import jax.numpy as jnp
from jax import lax
from jax.experimental import pallas as pl
from jax.experimental.pallas import tpu as pltpu
from jax.sharding import PartitionSpec as P

ROPE_BASE = 10000.0
NORM_EPS = 1e-6
NEG_BIG = -1e30
POS_BIG = 3e38
TP = 4
CTX = 4
PIECE = 128
NOPE = 128
ROPE = 64
VALUE = 128
GROUP = 4
DOWN_BLK = 512
COL_BLK = 256
O_SLOTS = 3
FIRST_EVENT = 3
SUM_LAG = 2
BACK_LAG = 3
RELAY_AT = 5
MESH_ID = pl.DeviceIdType.MESH


def rope_tables(pos_vals, copies):
    half_dim = ROPE // 2
    inv_freq = ROPE_BASE ** (-jnp.arange(half_dim, dtype=jnp.float32) * 2.0 / ROPE)
    angles = pos_vals.astype(jnp.float32)[..., None] * inv_freq
    cos_t, sin_t = jnp.cos(angles), jnp.sin(angles)
    return (jnp.concatenate([cos_t, cos_t] * copies, axis=-1),
            jnp.concatenate([-sin_t, sin_t] * copies, axis=-1))


def rms_norm(act_in, gain_row):
    inv_rms = lax.rsqrt(jnp.mean(act_in * act_in, axis=-1, keepdims=True) + NORM_EPS)
    return act_in * inv_rms * gain_row


def rotate(rows, cos_t, sin_t):
    width = rows.shape[1]
    lane = lax.broadcasted_iota(jnp.int32, rows.shape, 1)
    swapped = jnp.where(lax.rem(lane, ROPE) < ROPE // 2,
                        pltpu.roll(rows, width - ROPE // 2, 1), pltpu.roll(rows, ROPE // 2, 1))
    return rows * cos_t + swapped * sin_t


def layer_kernel(x_hbm, cos_ref, sin_ref, gq_ref, gkv_ref, wdq_hbm, wuq_hbm, wqr_hbm, wdkv_hbm, wkr_hbm, wuk_hbm, wuv_hbm, wo_hbm,
                 y_ref,
                 x_ref, wkr_ref, wdown, wq, wqr, wkv, wo,
                 lat, kpe, cq_f, cq, qn, qp, cap, o_ref, acc, rbuf,
                 x_sem, kr_sem, down_sem, q_sem, kv_sem, o_sem,
                 lat_send, lat_recv, f_send, f_recv, b_send, b_recv):
    my_tp = lax.axis_index('tp')
    my_ctx = lax.axis_index('ctx')
    n_rows, n_cols = y_ref.shape
    heads = o_ref.shape[1] // VALUE
    groups = heads // GROUP
    q_rank = cq.shape[1]
    lat_rank = wkv.shape[2]
    n_keys = 2 * CTX * PIECE
    low_keys = CTX * PIECE
    n_down = 1 + q_rank // DOWN_BLK
    left = lax.rem(my_tp + TP - 1, TP)
    right = lax.rem(my_tp + 1, TP)
    partner = my_ctx + 1 - 2 * lax.rem(my_ctx, 2)
    across = lax.rem(my_ctx + 2, CTX)

    x_copy = pltpu.make_async_copy(x_hbm, x_ref, x_sem)
    kr_copy = pltpu.make_async_copy(wkr_hbm, wkr_ref, kr_sem)

    def dq_copy(blk):
        cols = pl.ds(pl.multiple_of((blk - 1) * DOWN_BLK, DOWN_BLK), DOWN_BLK)
        slot = lax.rem(blk, 2)
        return pltpu.make_async_copy(wdq_hbm.at[:, cols], wdown.at[slot], down_sem.at[slot])

    dkv_copy = pltpu.make_async_copy(wdkv_hbm, wdown.at[0], down_sem.at[0])

    def q_copies(grp):
        slot = lax.rem(grp, 2)
        n_blk, r_blk = GROUP * NOPE, GROUP * ROPE
        return (pltpu.make_async_copy(wuq_hbm.at[:, pl.ds(pl.multiple_of(grp * n_blk, n_blk), n_blk)], wq.at[slot], q_sem.at[slot, 0]),
                pltpu.make_async_copy(wqr_hbm.at[:, pl.ds(pl.multiple_of(grp * r_blk, r_blk), r_blk)], wqr.at[slot], q_sem.at[slot, 1]))

    def kv_copies(grp):
        slot = lax.rem(grp, 2)
        n_blk = GROUP * NOPE
        cols = pl.ds(pl.multiple_of(grp * n_blk, n_blk), n_blk)
        return (pltpu.make_async_copy(wuk_hbm.at[:, cols], wkv.at[slot, 0], kv_sem.at[slot, 0]),
                pltpu.make_async_copy(wuv_hbm.at[:, cols], wkv.at[slot, 1], kv_sem.at[slot, 1]))

    row_blks = n_rows // PIECE
    half_cols = n_cols // 2
    col_steps = half_cols // COL_BLK
    n_chunks = col_steps * row_blks

    def o_copies(step):
        slot = lax.rem(step, O_SLOTS)
        return [pltpu.make_async_copy(
            wo_hbm.at[:, pl.ds(pl.multiple_of(side * half_cols + step * COL_BLK, COL_BLK), COL_BLK)],
            wo.at[slot, :, pl.ds(side * COL_BLK, COL_BLK)], o_sem.at[slot, side]) for side in range(2)]

    def start_all(copies):
        for copy in copies:
            copy.start()

    def wait_all(copies):
        for copy in copies:
            copy.wait()

    x_copy.start()
    kr_copy.start()
    dkv_copy.start()
    dq_copy(1).start()

    barrier = pltpu.get_barrier_semaphore()
    for peer in (partner, across):
        pl.semaphore_signal(barrier, inc=1, device_id={'ctx': peer}, device_id_type=MESH_ID)

    @pl.when(my_tp > 0)
    def _():
        pl.semaphore_signal(barrier, inc=1, device_id={'tp': left}, device_id_type=MESH_ID)

    @pl.when(my_tp < TP - 1)
    def _():
        pl.semaphore_signal(barrier, inc=1, device_id={'tp': right}, device_id_type=MESH_ID)

    for half, width in ((0, low_keys), (1, n_keys)):
        q_rank_of = (my_ctx if half == 0 else 2 * CTX - 1 - my_ctx) * PIECE + lax.broadcasted_iota(jnp.int32, (PIECE, width), 0)
        key = lax.broadcasted_iota(jnp.int32, (PIECE, width), 1)
        up_piece = 2 * CTX - 1 - (key - low_keys) // PIECE
        k_rank_of = jnp.where(key < low_keys, key, up_piece * PIECE + lax.rem(key, PIECE))
        start = 0 if half == 0 else low_keys
        cap[:, start:start + width] = jnp.where(k_rank_of <= q_rank_of, POS_BIG, NEG_BIG)

    x_copy.wait()
    kr_copy.wait()
    rot = jnp.dot(x_ref[...], wkr_ref[...], preferred_element_type=jnp.float32)
    rot = jnp.concatenate([rot, rot], axis=1)
    k_rot = rotate(rot, cos_ref[:, :2 * ROPE], sin_ref[:, :2 * ROPE]).astype(jnp.bfloat16)
    dkv_copy.wait()
    c_kv = rms_norm(jnp.dot(x_ref[...], wdown[0], preferred_element_type=jnp.float32), gkv_ref[...]).astype(jnp.bfloat16)
    for half in range(2):
        rows = slice(half * PIECE, (half + 1) * PIECE)
        lat[half, my_ctx, :, :lat_rank] = c_kv[rows]
        lat[half, my_ctx, :, lat_rank:] = k_rot[rows]

    @pl.when((my_tp > 0) & (my_tp < TP - 1))
    def _():
        pl.semaphore_wait(barrier, 4)

    @pl.when((my_tp == 0) | (my_tp == TP - 1))
    def _():
        pl.semaphore_wait(barrier, 3)

    def lat_copy(owner, peer, sem):
        part = lat.at[:, owner]
        return pltpu.make_async_remote_copy(src_ref=part, dst_ref=part, send_sem=lat_send.at[sem], recv_sem=lat_recv.at[sem],
                                            device_id={'ctx': peer}, device_id_type=MESH_ID)

    lat_copy(my_ctx, across, 1).start()
    lat_copy(my_ctx, partner, 0).start()

    def dq_step(blk, _):
        @pl.when(blk + 1 < n_down)
        def _():
            dq_copy(blk + 1).start()

        @pl.when(blk + 1 == n_down)
        def _():
            start_all(q_copies(0))
            start_all(q_copies(1))

        dq_copy(blk).wait()
        cols = pl.ds(pl.multiple_of((blk - 1) * DOWN_BLK, DOWN_BLK), DOWN_BLK)
        cq_f[:, cols] = jnp.dot(x_ref[...], wdown[lax.rem(blk, 2)], preferred_element_type=jnp.float32)
        return 0

    lax.fori_loop(1, n_down, dq_step, 0)
    cq[...] = rms_norm(cq_f[...], gq_ref[...]).astype(jnp.bfloat16)

    def q_step(grp, _):
        slot = lax.rem(grp, 2)
        wait_all(q_copies(grp))
        qn[grp] = jnp.dot(cq[...], wq[slot], preferred_element_type=jnp.float32).astype(jnp.bfloat16)
        q_rot = jnp.dot(cq[...], wqr[slot], preferred_element_type=jnp.float32)
        qp[grp] = rotate(q_rot, cos_ref[...], sin_ref[...]).astype(jnp.bfloat16)

        @pl.when(grp + 2 < groups)
        def _():
            start_all(q_copies(grp + 2))

        @pl.when(grp + 2 == groups)
        def _():
            start_all(kv_copies(0))
            start_all(kv_copies(1))

        @pl.when(grp == RELAY_AT)
        def _():
            lat_copy(across, across, 1).wait_recv()
            lat_copy(across, partner, 2).start()
        return 0

    lax.fori_loop(0, groups, q_step, 0)
    for step in range(O_SLOTS - 1):
        start_all(o_copies(step))
    lat_copy(partner, partner, 0).wait_recv()
    lat_copy(across, partner, 2).wait_recv()

    lane = lax.broadcasted_iota(jnp.int32, (n_keys, 2 * ROPE), 1)
    both = lat[:, :, :, lat_rank:].reshape(n_keys, 2 * ROPE)
    zero = jnp.zeros_like(both)
    kpe[0] = jnp.where(lane < ROPE, both, zero)
    kpe[1] = jnp.where(lane < ROPE, zero, both)

    expo_scale = (NOPE + ROPE) ** -0.5 * math.log2(math.e)
    nt = (((1,), (1,)), ((), ()))

    def attend(scores, caps, values):
        scores = jnp.minimum(scores, caps)
        top = jnp.max(scores, axis=-1, keepdims=True)
        prob = jnp.exp2((scores - top) * expo_scale)
        total = jnp.sum(prob, axis=-1, keepdims=True)
        out = jnp.dot(prob.astype(jnp.bfloat16), values, preferred_element_type=jnp.float32)
        return (out / total).astype(jnp.bfloat16)

    def head_step(grp, _):
        slot = lax.rem(grp, 2)
        wait_all(kv_copies(grp))
        c_all = lat[:, :, :, :lat_rank].reshape(n_keys, lat_rank)
        k_all = jnp.dot(c_all, wkv[slot, 0], preferred_element_type=jnp.float32).astype(jnp.bfloat16)
        v_all = jnp.dot(c_all, wkv[slot, 1], preferred_element_type=jnp.float32).astype(jnp.bfloat16)

        @pl.when(grp + 2 < groups)
        def _():
            start_all(kv_copies(grp + 2))

        for head in range(GROUP):
            cols = slice(head * NOPE, (head + 1) * NOPE)
            pair = slice((head // 2) * 2 * ROPE, (head // 2 + 1) * 2 * ROPE)
            q_cat = jnp.concatenate([qn[grp, :, cols], qp[grp, :, pair]], axis=1)
            k_cat = jnp.concatenate([k_all[:, cols], kpe[head % 2]], axis=1)
            v_head = v_all[:, cols]
            s_low = lax.dot_general(q_cat, k_cat[:low_keys], nt, preferred_element_type=jnp.float32)
            s_up = lax.dot_general(q_cat[PIECE:], k_cat[low_keys:], nt, preferred_element_type=jnp.float32)
            out_cols = pl.ds(pl.multiple_of(grp * (GROUP * VALUE), GROUP * VALUE) + head * VALUE, VALUE)
            o_ref[:PIECE, out_cols] = attend(s_low[:PIECE], cap[:, :low_keys], v_head[:low_keys])
            s_both = jnp.concatenate([s_low[PIECE:], s_up], axis=1)
            o_ref[PIECE:, out_cols] = attend(s_both, cap[:, low_keys:], v_head)
        return 0

    lax.fori_loop(0, groups, head_step, 0)

    depth = (TP - 1 - my_tp, my_tp)
    onward = (left, right)
    back = (right, left)

    def y_slice(side, chunk):
        step, row = chunk // row_blks, lax.rem(chunk, row_blks)
        return (pl.ds(pl.multiple_of(row * PIECE, PIECE), PIECE),
                pl.ds(pl.multiple_of(side * half_cols + step * COL_BLK, COL_BLK), COL_BLK))

    def f_copy(side, chunk):
        return pltpu.make_async_remote_copy(
            src_ref=acc.at[side, chunk], dst_ref=rbuf.at[side, chunk],
            send_sem=f_send.at[side, chunk], recv_sem=f_recv.at[side, chunk],
            device_id={'tp': onward[side]}, device_id_type=MESH_ID)

    def b_copy(side, chunk):
        part = y_ref.at[y_slice(side, chunk)]
        return pltpu.make_async_remote_copy(
            src_ref=part, dst_ref=part,
            send_sem=b_send.at[side, chunk], recv_sem=b_recv.at[side, chunk],
            device_id={'tp': back[side]}, device_id_type=MESH_ID)

    def reduce_event(side, event):
        chunk = event - SUM_LAG * (depth[side] - 1)
        live = (chunk >= 0) & (chunk < n_chunks)

        @pl.when(live & (depth[side] > 0))
        def _():
            f_copy(side, chunk).wait_recv()

        @pl.when(live & (depth[side] > 0) & (depth[side] < TP - 1))
        def _():
            acc[side, chunk] = acc[side, chunk] + rbuf[side, chunk]
            f_copy(side, chunk).start()

        @pl.when(live & (depth[side] == TP - 1))
        def _():
            total = acc[side, chunk] + rbuf[side, chunk]
            y_ref[y_slice(side, chunk)] = total.astype(y_ref.dtype)
            b_copy(side, chunk).start()

    def out_step(step, _):
        slot = lax.rem(step, O_SLOTS)

        @pl.when(step + O_SLOTS - 1 < col_steps)
        def _():
            start_all(o_copies(step + O_SLOTS - 1))

        wait_all(o_copies(step))
        part = jnp.dot(o_ref[...], wo[slot], preferred_element_type=jnp.float32)
        for side in range(2):
            for row in range(row_blks):
                chunk = step * row_blks + row
                acc[side, chunk] = part[row * PIECE:(row + 1) * PIECE, side * COL_BLK:(side + 1) * COL_BLK]

                @pl.when(depth[side] == 0)
                def _():
                    f_copy(side, chunk).start()

        @pl.when(step >= FIRST_EVENT)
        def _():
            for side in range(2):
                reduce_event(side, step - FIRST_EVENT)
        return 0

    lax.fori_loop(0, col_steps, out_step, 0)

    def late_event(event, _):
        for side in range(2):
            reduce_event(side, event)
        return 0

    lax.fori_loop(col_steps - FIRST_EVENT, n_chunks + SUM_LAG * (TP - 2), late_event, 0)

    def back_event(event, _):
        for side in range(2):
            chunk = event - BACK_LAG * (TP - 2 - depth[side])
            live = (chunk >= 0) & (chunk < n_chunks)

            @pl.when(live & (depth[side] < TP - 1))
            def _():
                b_copy(side, chunk).wait_recv()

            @pl.when(live & (depth[side] > 0) & (depth[side] < TP - 1))
            def _():
                b_copy(side, chunk).start()
        return 0

    lax.fori_loop(0, n_chunks + BACK_LAG * (TP - 2), back_event, 0)

    lat_copy(my_ctx, partner, 0).wait_send()
    lat_copy(my_ctx, across, 1).wait_send()
    lat_copy(across, partner, 2).wait_send()

    def drain(chunk, _):
        for side in range(2):
            @pl.when(depth[side] < TP - 1)
            def _():
                f_copy(side, chunk).wait_send()

            @pl.when(depth[side] > 0)
            def _():
                b_copy(side, chunk).wait_send()
        return 0

    lax.fori_loop(0, n_chunks, drain, 0)


def layer(tok_x, tok_pos, w_dq, g_q, w_uq, w_qr, w_dkv, g_kv, w_kr, w_uk, w_uv, w_o):
    n_rows, model_dim = tok_x.shape
    q_rank, lat_rank = w_dq.shape[1], w_dkv.shape[1]
    heads = w_uq.shape[1] // NOPE
    groups = heads // GROUP
    n_keys = CTX * n_rows
    n_chunks = (model_dim // 2 // COL_BLK) * (n_rows // PIECE)
    bf16, f32 = jnp.bfloat16, jnp.float32
    cos_t, sin_t = rope_tables(tok_pos, GROUP)
    vmem = pl.BlockSpec(memory_space=pltpu.VMEM)
    hbm = pl.BlockSpec(memory_space=pl.ANY)
    dma = pltpu.SemaphoreType.DMA
    return pl.pallas_call(
        layer_kernel,
        out_shape=jax.ShapeDtypeStruct((n_rows, model_dim), bf16),
        in_specs=[hbm, vmem, vmem, vmem, vmem] + [hbm] * 8,
        out_specs=vmem,
        scratch_shapes=[
            pltpu.VMEM((n_rows, model_dim), bf16),
            pltpu.VMEM((model_dim, ROPE), bf16),
            pltpu.VMEM((2, model_dim, DOWN_BLK), bf16),
            pltpu.VMEM((2, q_rank, GROUP * NOPE), bf16),
            pltpu.VMEM((2, q_rank, GROUP * ROPE), bf16),
            pltpu.VMEM((2, 2, lat_rank, GROUP * NOPE), bf16),
            pltpu.VMEM((O_SLOTS, heads * VALUE, 2 * COL_BLK), bf16),
            pltpu.VMEM((2, CTX, PIECE, lat_rank + 2 * ROPE), bf16),
            pltpu.VMEM((2, n_keys, 2 * ROPE), bf16),
            pltpu.VMEM((n_rows, q_rank), f32),
            pltpu.VMEM((n_rows, q_rank), bf16),
            pltpu.VMEM((groups, n_rows, GROUP * NOPE), bf16),
            pltpu.VMEM((groups, n_rows, GROUP * ROPE), bf16),
            pltpu.VMEM((PIECE, n_keys // 2 + n_keys), f32),
            pltpu.VMEM((n_rows, heads * VALUE), bf16),
            pltpu.VMEM((2, n_chunks, PIECE, COL_BLK), f32),
            pltpu.VMEM((2, n_chunks, PIECE, COL_BLK), f32),
            dma, dma, dma((2,)), dma((2, 2)), dma((2, 2)), dma((O_SLOTS, 2)),
            dma((3,)), dma((3,)),
            dma((2, n_chunks)), dma((2, n_chunks)), dma((2, n_chunks)), dma((2, n_chunks)),
        ],
        compiler_params=pltpu.CompilerParams(collective_id=0, has_side_effects=True, vmem_limit_bytes=67043328),
        name='layer',
    )(tok_x, cos_t, sin_t, g_q.astype(f32)[None], g_kv.astype(f32)[None], w_dq, w_uq, w_qr, w_dkv, w_kr, w_uk, w_uv, w_o)


def solution(mesh):
    tok_spec = P(('dp', 'ctx'), None)
    pos_spec = P(('dp', 'ctx'))
    full_mat = P(None, None)
    full_vec = P(None)
    col_spec = P(None, 'tp')
    row_spec = P('tp', None)
    return jax.shard_map(layer, mesh=mesh,
                         in_specs=(tok_spec, pos_spec, full_mat, full_vec, col_spec, col_spec, full_mat, full_vec, full_mat, col_spec, col_spec, row_spec),
                         out_specs=tok_spec, check_vma=False)
```

time: 221 us -> 166 us (0.75)
  matrix products: 61.5 us -> 0 us
  Pallas kernels: 108 us -> 154 us
  other arithmetic: 16 us -> 2.5 us
  waiting for transfers between devices: 10.2 us -> 0 us
  starting transfers between devices: 9.03 us -> 0 us
  local copies, waits for them, and re-layouts: 15.6 us -> 8.97 us
    dot_general x25 -> x0, matrix products: 61.5 us -> none  [the longest x4 11.9 us: block_stats(): jnp.einsum('hqk,khv->hqv', prob_tile.astype(jnp.bfloat16), v_rows, prefer...]
    pallas_call x1, Pallas kernels: 108 us -> 154 us  [layer(): pl.pallas_call(layer_kernel, out_shape=jax.ShapeDtypeStruct((n_rows, mode...]
    ppermute x6 -> x0, waiting for transfers between devices: 10.2 us -> none  [the longest x3 10.2 us: ctx_step(): rot_blk = lax.ppermute(rot_blk, 'ctx', next_perm)]
    ppermute x6 -> x0, starting transfers between devices: 9.03 us -> none  [the longest x3 7.93 us: ctx_step(): rot_blk = lax.ppermute(rot_blk, 'ctx', next_perm)]
    concatenate x8 -> x0, other arithmetic: 8.35 us -> none  [the longest x3 7.27 us: attend_upper(): jnp.concatenate([old_acc[:, :half_len], top_acc], axis=1)]
    cond x12 -> x0, local copies, waits for them, and re-layouts: 6.84 us -> none
    reduce_sum x4 -> x0, other arithmetic: 3.92 us -> none  [block_stats(): blk_sum = jnp.sum(prob_tile, axis=-1)]
    reshape x1 -> x0, other arithmetic: 2.88 us -> none  [local_step(): attn_out.transpose(1, 0, 2).reshape(tok_x.shape[0], heads_loc * value_dim)]
  transfers between devices with their start and end apart: 6 -> 0, of which waited for: 3 -> 0; matrix products, arithmetic and copies ran while one was open for 0% -> 0% of each run, Pallas kernels for 0% -> 0%
where the time goes in v3:
time: 166 us; the launch traced here: 165 us
  Pallas kernels  154 us (93%)
  local copies, waits for them, and re-layouts  8.97 us (5%)
  other arithmetic  2.5 us (2%)
    pallas_call x1, Pallas kernels, layer(): pl.pallas_call(layer_kernel, out_shape=jax.ShapeDtypeStruct((n_rows, mode...  154 us
    unnamed x2, local copies, waits for them, and re-layouts  5.71 us

profile of v3, /device:TPU:0, one launch (start us, length us, event | category | flops | bytes accessed | tf_op | source)
XLA Modules:
  0.0 165.2 jit_solution(12999520334444535030)
XLA Ops:
  0.0 0.7 convert_element_type.2
  0.7 1.3 broadcast_in_dim.17
  2.0 1.3 reshape.7.gq_ref
  3.2 0.5 multiply_sine_fusion
  3.8 1.0 concatenate.7.sin_ref
  4.8 1.0 concatenate.6.cos_ref
  5.8 2.3 %copy.15.wkr_hbm = bf16[5120,64]{1,0:T(8,128)(2,1)} copy(bf16[5120,64]{0,1:T(8,128)(2,1)} %param.20) | data formatting | bytes 1310720 | tf_op args[8]
  8.1 153.7 %layer.1 = bf16[256,5120]{1,0:T(8,128)(2,1)} custom-call(bf16[256,5120]{1,0:T(8,128)(2,1)} %x_hbm.1, f32[256,256]{1,0:T(8,128)} %concatenate.6.cos_ref, f32[256,256]{1,0:T(8,128)} %concatenate.7.sin_ref, f32[1,1536]{1,0:T(1,128)} %reshape.7.gq_ref, f32[1,512]{1,0:T(1,128)} %bitcast.1, bf16[5120,1536]{1,0:T(8,128)(2,1)} %wdq_hbm.1, ...), custom_call_target="tpu_custom_call" | custom-call | tf_op jit(solution)/shard_map/layer/pallas_call | solution.py:379
  161.8 3.4 %copy.17 = bf16[256,5120]{1,0:T(8,128)(2,1)} copy(bf16[256,5120]{1,0:T(8,128)(2,1)} %layer.1) | data formatting | bytes 5242880
  (1 shorter events, 0.0 us)

commit v4 on v3

v4 whole, which is shorter than its diff:
```python
import math

import jax
import jax.numpy as jnp
import numpy as np
from jax import lax
from jax.experimental import pallas as pl
from jax.experimental.pallas import tpu as pltpu
from jax.sharding import PartitionSpec as P

ROPE_BASE = 10000.0
NORM_EPS = 1e-6
NEG_BIG = -1e30
POS_BIG = 3e38
TP = 4
CTX = 4
PIECE = 128
NOPE = 128
ROPE = 64
VALUE = 128
GROUP = 4
DOWN_BLK = 512
COL_BLK = 256
O_SLOTS = 3
LOW_FIRST = 4
HIGH_FIRST = 5
EVENTS_OUT = 3
SUM_LAG = 2
BACK_LAG = 3
MESH_ID = pl.DeviceIdType.MESH


def inv_freq_row():
    half_dim = ROPE // 2
    inv_freq = np.float32(ROPE_BASE) ** (-np.arange(half_dim, dtype=np.float32) * np.float32(2.0) / np.float32(ROPE))
    return np.tile(inv_freq.astype(np.float32), 4)[None]


def rms_norm(act_in, gain_row):
    inv_rms = lax.rsqrt(jnp.mean(act_in * act_in, axis=-1, keepdims=True) + NORM_EPS)
    return act_in * inv_rms * gain_row


def rotate(rows, cos_t, sin_t):
    width = rows.shape[1]
    lane = lax.broadcasted_iota(jnp.int32, rows.shape, 1)
    swapped = jnp.where(lax.rem(lane, ROPE) < ROPE // 2,
                        pltpu.roll(rows, width - ROPE // 2, 1), pltpu.roll(rows, ROPE // 2, 1))
    return rows * cos_t + swapped * sin_t


def layer_kernel(x_hbm, pos_ref, freq_ref, gq_ref, gkv_ref, wdq_hbm, wuq_hbm, wqr_hbm, wdkv_hbm, wkr_hbm, wuk_hbm, wuv_hbm, wo_hbm,
                 y_ref,
                 x_ref, wkr_ref, wbig, wq, wqr, wkv,
                 cos_ref, sin_ref, lat, kpe, cq_f, cq, qn, qp, kv_low, cap, o_ref, acc, rbuf,
                 x_sem, kr_sem, down_sem, q_sem, kv_sem, o_sem,
                 lat_send, lat_recv, f_send, f_recv, b_send, b_recv):
    my_tp = lax.axis_index('tp')
    my_ctx = lax.axis_index('ctx')
    n_rows, n_cols = y_ref.shape
    heads = o_ref.shape[1] // VALUE
    groups = heads // GROUP
    q_rank = cq.shape[1]
    lat_rank = wkv.shape[2]
    n_keys = 2 * CTX * PIECE
    low_keys = CTX * PIECE
    n_down = 1 + q_rank // DOWN_BLK
    left = lax.rem(my_tp + TP - 1, TP)
    right = lax.rem(my_tp + 1, TP)
    partner = my_ctx + 1 - 2 * lax.rem(my_ctx, 2)
    across = lax.rem(my_ctx + 2, CTX)

    x_copy = pltpu.make_async_copy(x_hbm, x_ref, x_sem)
    kr_copy = pltpu.make_async_copy(wkr_hbm, wkr_ref, kr_sem)

    def dq_copy(blk):
        cols = pl.ds(pl.multiple_of((blk - 1) * DOWN_BLK, DOWN_BLK), DOWN_BLK)
        slot = lax.rem(blk, 2)
        return pltpu.make_async_copy(wdq_hbm.at[:, cols], wbig.at[slot], down_sem.at[slot])

    dkv_copy = pltpu.make_async_copy(wdkv_hbm, wbig.at[0], down_sem.at[0])

    def q_copies(grp):
        slot = lax.rem(grp, 2)
        n_blk, r_blk = GROUP * NOPE, GROUP * ROPE
        return (pltpu.make_async_copy(wuq_hbm.at[:, pl.ds(pl.multiple_of(grp * n_blk, n_blk), n_blk)], wq.at[slot], q_sem.at[slot, 0]),
                pltpu.make_async_copy(wqr_hbm.at[:, pl.ds(pl.multiple_of(grp * r_blk, r_blk), r_blk)], wqr.at[slot], q_sem.at[slot, 1]))

    def kv_copies(turn):
        grp, slot = lax.rem(turn, groups), lax.rem(turn, 2)
        n_blk = GROUP * NOPE
        cols = pl.ds(pl.multiple_of(grp * n_blk, n_blk), n_blk)
        return (pltpu.make_async_copy(wuk_hbm.at[:, cols], wkv.at[slot, 0], kv_sem.at[slot, 0]),
                pltpu.make_async_copy(wuv_hbm.at[:, cols], wkv.at[slot, 1], kv_sem.at[slot, 1]))

    row_blks = n_rows // PIECE
    half_cols = n_cols // 2
    col_steps = half_cols // COL_BLK
    n_chunks = col_steps * row_blks

    def o_copies(turn):
        step, slot = lax.rem(turn, col_steps), lax.rem(turn, O_SLOTS)
        return [pltpu.make_async_copy(
            wo_hbm.at[:, pl.ds(pl.multiple_of(side * half_cols + step * COL_BLK, COL_BLK), COL_BLK)],
            wbig.at[slot, pl.ds(0, heads * VALUE), pl.ds(side * COL_BLK, COL_BLK)], o_sem.at[slot, side]) for side in range(2)]

    def start_all(copies):
        for copy in copies:
            copy.start()

    def wait_all(copies):
        for copy in copies:
            copy.wait()

    x_copy.start()
    kr_copy.start()
    dkv_copy.start()
    dq_copy(1).start()

    barrier = pltpu.get_barrier_semaphore()
    for peer in (partner, across):
        pl.semaphore_signal(barrier, inc=1, device_id={'ctx': peer}, device_id_type=MESH_ID)

    @pl.when(my_tp > 0)
    def _():
        pl.semaphore_signal(barrier, inc=1, device_id={'tp': left}, device_id_type=MESH_ID)

    @pl.when(my_tp < TP - 1)
    def _():
        pl.semaphore_signal(barrier, inc=1, device_id={'tp': right}, device_id_type=MESH_ID)

    row = lax.broadcasted_iota(jnp.int32, (n_rows, n_rows), 0)
    col = lax.broadcasted_iota(jnp.int32, (n_rows, n_rows), 1)
    pos_row = pos_ref[...].astype(jnp.float32).reshape(1, n_rows)
    pos_col = jnp.sum(jnp.where(row == col, pos_row, 0.0), axis=1, keepdims=True)
    angles = pos_col * freq_ref[...]
    lane_of = lax.broadcasted_iota(jnp.int32, angles.shape, 1)
    cos_t = jnp.cos(angles)
    sin_t = jnp.where(lax.rem(lane_of, ROPE) < ROPE // 2, -1.0, 1.0) * jnp.sin(angles)
    for copy in range(GROUP // 2):
        cos_ref[:, copy * 2 * ROPE:(copy + 1) * 2 * ROPE] = cos_t
        sin_ref[:, copy * 2 * ROPE:(copy + 1) * 2 * ROPE] = sin_t

    for half, width in ((0, low_keys), (1, n_keys)):
        q_rank_of = (my_ctx if half == 0 else 2 * CTX - 1 - my_ctx) * PIECE + lax.broadcasted_iota(jnp.int32, (PIECE, width), 0)
        key = lax.broadcasted_iota(jnp.int32, (PIECE, width), 1)
        up_piece = 2 * CTX - 1 - (key - low_keys) // PIECE
        k_rank_of = jnp.where(key < low_keys, key, up_piece * PIECE + lax.rem(key, PIECE))
        start = 0 if half == 0 else low_keys
        cap[:, start:start + width] = jnp.where(k_rank_of <= q_rank_of, POS_BIG, NEG_BIG)

    x_copy.wait()
    kr_copy.wait()
    rot = lax.dot_general(x_ref[...], wkr_ref[...], (((1,), (1,)), ((), ())), preferred_element_type=jnp.float32)
    rot = jnp.concatenate([rot, rot], axis=1)
    k_rot = rotate(rot, cos_ref[:, :2 * ROPE], sin_ref[:, :2 * ROPE]).astype(jnp.bfloat16)
    dkv_copy.wait()
    c_kv = rms_norm(jnp.dot(x_ref[...], wbig[0], preferred_element_type=jnp.float32), gkv_ref[...].astype(jnp.float32).reshape(1, lat_rank)).astype(jnp.bfloat16)
    for half in range(2):
        rows = slice(half * PIECE, (half + 1) * PIECE)
        lat[half, my_ctx, :, :lat_rank] = c_kv[rows]
        lat[half, my_ctx, :, lat_rank:] = k_rot[rows]

    @pl.when((my_tp > 0) & (my_tp < TP - 1))
    def _():
        pl.semaphore_wait(barrier, 4)

    @pl.when((my_tp == 0) | (my_tp == TP - 1))
    def _():
        pl.semaphore_wait(barrier, 3)

    def lat_copy(owner, peer, sem):
        part = lat.at[:, owner]
        return pltpu.make_async_remote_copy(src_ref=part, dst_ref=part, send_sem=lat_send.at[sem], recv_sem=lat_recv.at[sem],
                                            device_id={'ctx': peer}, device_id_type=MESH_ID)

    lat_copy(my_ctx, across, 1).start()
    lat_copy(my_ctx, partner, 0).start()

    def dq_step(blk, _):
        @pl.when(blk + 1 < n_down)
        def _():
            dq_copy(blk + 1).start()

        @pl.when(blk + 1 == n_down)
        def _():
            for grp in range(2):
                start_all(q_copies(grp))
                start_all(kv_copies(grp))

        dq_copy(blk).wait()
        cols = pl.ds(pl.multiple_of((blk - 1) * DOWN_BLK, DOWN_BLK), DOWN_BLK)
        cq_f[:, cols] = jnp.dot(x_ref[...], wbig[lax.rem(blk, 2)], preferred_element_type=jnp.float32)
        return 0

    lax.fori_loop(1, n_down, dq_step, 0)
    cq[...] = rms_norm(cq_f[...], gq_ref[...].astype(jnp.float32).reshape(1, q_rank)).astype(jnp.bfloat16)

    for turn in range(O_SLOTS - 1):
        start_all(o_copies(turn))

    lat_copy(across, across, 1).wait_recv()
    lat_copy(across, partner, 2).start()
    lat_copy(partner, partner, 0).wait_recv()
    lat_copy(across, partner, 2).wait_recv()

    lane = lax.broadcasted_iota(jnp.int32, (n_keys, 2 * ROPE), 1)
    k_rots = lat[:, :, :, lat_rank:].reshape(n_keys, 2 * ROPE)
    zero = jnp.zeros_like(k_rots)
    kpe[0] = jnp.where(lane < ROPE, k_rots, zero)
    kpe[1] = jnp.where(lane < ROPE, zero, k_rots)

    expo_scale = (NOPE + ROPE) ** -0.5 * math.log2(math.e)

    def attend(q_nope, q_rot, keys, k_rots, values, caps):
        k_cat = jnp.concatenate([keys, k_rots], axis=1)
        q_cat = jnp.concatenate([q_nope, q_rot], axis=1)
        scores = lax.dot_general(q_cat, k_cat, (((1,), (1,)), ((), ())), preferred_element_type=jnp.float32)
        scores = jnp.minimum(scores, caps)
        top = jnp.max(scores, axis=-1, keepdims=True)
        prob = jnp.exp2((scores - top) * expo_scale)
        total = jnp.sum(prob, axis=-1, keepdims=True)
        out = jnp.dot(prob.astype(jnp.bfloat16), values, preferred_element_type=jnp.float32)
        return (out / total).astype(jnp.bfloat16)

    def up_project(half, slot):
        rows = lat[half, :, :, :lat_rank].reshape(low_keys, lat_rank)
        return [jnp.dot(rows, wkv[slot, part], preferred_element_type=jnp.float32).astype(jnp.bfloat16) for part in range(2)]

    def out_cols(grp, head):
        return pl.ds(pl.multiple_of(grp * (GROUP * VALUE), GROUP * VALUE) + head * VALUE, VALUE)

    def low_step(grp, _):
        slot = lax.rem(grp, 2)
        wait_all(q_copies(grp))
        wait_all(kv_copies(grp))
        q_nope = jnp.dot(cq[...], wq[slot], preferred_element_type=jnp.float32).astype(jnp.bfloat16)
        q_rot = jnp.dot(cq[...], wqr[slot], preferred_element_type=jnp.float32)
        q_rot = rotate(q_rot, cos_ref[...], sin_ref[...]).astype(jnp.bfloat16)
        qn[grp] = q_nope[PIECE:]
        qp[grp] = q_rot[PIECE:]
        k_low, v_low = up_project(0, slot)
        kv_low[grp, 0] = k_low
        kv_low[grp, 1] = v_low
        for head in range(GROUP):
            cols = slice(head * NOPE, (head + 1) * NOPE)
            pair = slice((head // 2) * 2 * ROPE, (head // 2 + 1) * 2 * ROPE)
            o_ref[:PIECE, out_cols(grp, head)] = attend(
                q_nope[:PIECE, cols], q_rot[:PIECE, pair], k_low[:, cols], kpe[head % 2, :low_keys], v_low[:, cols], cap[:, :low_keys])

        start_all(kv_copies(grp + 2))

        @pl.when(grp + 2 < groups)
        def _():
            start_all(q_copies(grp + 2))
        return 0

    lax.fori_loop(0, groups, low_step, 0)

    def high_step(grp):
        slot = lax.rem(grp, 2)
        wait_all(kv_copies(groups + grp))
        k_up, v_up = up_project(1, slot)
        for head in range(GROUP):
            cols = slice(head * NOPE, (head + 1) * NOPE)
            pair = slice((head // 2) * 2 * ROPE, (head // 2 + 1) * 2 * ROPE)
            keys = jnp.concatenate([kv_low[grp, 0, :, cols], k_up[:, cols]], axis=0)
            values = jnp.concatenate([kv_low[grp, 1, :, cols], v_up[:, cols]], axis=0)
            o_ref[PIECE:, out_cols(grp, head)] = attend(
                qn[grp, :, cols], qp[grp, :, pair], keys, kpe[head % 2], values, cap[:, low_keys:])

        @pl.when(grp + 2 < groups)
        def _():
            start_all(kv_copies(groups + grp + 2))

    depth = (TP - 1 - my_tp, my_tp)
    onward = (left, right)
    back = (right, left)

    def y_slice(side, chunk):
        row, step = chunk // col_steps, lax.rem(chunk, col_steps)
        return (pl.ds(pl.multiple_of(row * PIECE, PIECE), PIECE),
                pl.ds(pl.multiple_of(side * half_cols + step * COL_BLK, COL_BLK), COL_BLK))

    def f_copy(side, chunk):
        return pltpu.make_async_remote_copy(
            src_ref=acc.at[side, chunk], dst_ref=rbuf.at[side, chunk],
            send_sem=f_send.at[side, chunk], recv_sem=f_recv.at[side, chunk],
            device_id={'tp': onward[side]}, device_id_type=MESH_ID)

    def b_copy(side, chunk):
        part = y_ref.at[y_slice(side, chunk)]
        return pltpu.make_async_remote_copy(
            src_ref=part, dst_ref=part,
            send_sem=b_send.at[side, chunk], recv_sem=b_recv.at[side, chunk],
            device_id={'tp': back[side]}, device_id_type=MESH_ID)

    def reduce_event(side, event, row):
        chunk = event - SUM_LAG * (depth[side] - 1)
        live = (chunk >= 0) & (chunk < col_steps)
        chunk = chunk + row * col_steps

        @pl.when(live & (depth[side] > 0))
        def _():
            f_copy(side, chunk).wait_recv()

        @pl.when(live & (depth[side] > 0) & (depth[side] < TP - 1))
        def _():
            acc[side, chunk] = acc[side, chunk] + rbuf[side, chunk]
            f_copy(side, chunk).start()

        @pl.when(live & (depth[side] == TP - 1))
        def _():
            total = acc[side, chunk] + rbuf[side, chunk]
            y_ref[y_slice(side, chunk)] = total.astype(y_ref.dtype)
            b_copy(side, chunk).start()

    def back_event(side, event, row):
        chunk = event - BACK_LAG * (TP - 2 - depth[side])
        live = (chunk >= 0) & (chunk < col_steps)
        chunk = chunk + row * col_steps

        @pl.when(live & (depth[side] < TP - 1))
        def _():
            b_copy(side, chunk).wait_recv()

        @pl.when(live & (depth[side] > 0) & (depth[side] < TP - 1))
        def _():
            b_copy(side, chunk).start()

    def both(event_fn, event, row):
        for side in range(2):
            event_fn(side, event, row)

    def project(row, step):
        turn = row * col_steps + step

        @pl.when(turn + O_SLOTS - 1 < row_blks * col_steps)
        def _():
            start_all(o_copies(turn + O_SLOTS - 1))

        wait_all(o_copies(turn))
        part = jnp.dot(o_ref[row * PIECE:(row + 1) * PIECE], wbig[lax.rem(turn, O_SLOTS), :heads * VALUE], preferred_element_type=jnp.float32)
        for side in range(2):
            acc[side, turn] = part[:, side * COL_BLK:(side + 1) * COL_BLK]

            @pl.when(depth[side] == 0)
            def _():
                f_copy(side, turn).start()

    sum_events = col_steps + SUM_LAG * (TP - 2)
    back_events = col_steps + BACK_LAG * (TP - 2)

    def low_out(step, _):
        project(0, step)

        @pl.when((step >= LOW_FIRST) & (lax.rem(step, 2) == 0))
        def _():
            both(reduce_event, (step - LOW_FIRST) // 2, 0)
        return 0

    lax.fori_loop(0, col_steps, low_out, 0)

    def high_attention(grp, _):
        high_step(grp)

        @pl.when(lax.rem(grp, 4) != 3)
        def _():
            both(reduce_event, EVENTS_OUT + grp - grp // 4, 0)
        return 0

    lax.fori_loop(0, groups, high_attention, 0)

    first_sum = EVENTS_OUT + groups - groups // 4

    def high_out(step, _):
        project(1, step)

        @pl.when((lax.rem(step, 2) == 0) & (first_sum + step // 2 < sum_events))
        def _():
            both(reduce_event, first_sum + step // 2, 0)

        @pl.when(step >= HIGH_FIRST)
        def _():
            both(back_event, step - HIGH_FIRST, 0)
        return 0

    lax.fori_loop(0, col_steps, high_out, 0)

    first_back = col_steps - HIGH_FIRST
    for event in range(first_sum + (col_steps + 1) // 2, sum_events):
        both(reduce_event, event, 0)

    def high_sum(event, _):
        both(reduce_event, event, 1)

        @pl.when(first_back + event < back_events)
        def _():
            both(back_event, first_back + event, 0)
        return 0

    lax.fori_loop(0, sum_events, high_sum, 0)
    for event in range(first_back + sum_events, back_events):
        both(back_event, event, 0)

    def high_back(event, _):
        both(back_event, event, 1)
        return 0

    lax.fori_loop(0, back_events, high_back, 0)

    lat_copy(my_ctx, partner, 0).wait_send()
    lat_copy(my_ctx, across, 1).wait_send()
    lat_copy(across, partner, 2).wait_send()

    def drain(chunk, _):
        for side in range(2):
            @pl.when(depth[side] < TP - 1)
            def _():
                f_copy(side, chunk).wait_send()

            @pl.when(depth[side] > 0)
            def _():
                b_copy(side, chunk).wait_send()
        return 0

    lax.fori_loop(0, n_chunks, drain, 0)


def layer(tok_x, tok_pos, w_dq, g_q, w_uq, w_qr, w_dkv, g_kv, w_kr, w_uk, w_uv, w_o):
    n_rows, model_dim = tok_x.shape
    q_rank, lat_rank = w_dq.shape[1], w_dkv.shape[1]
    heads = w_uq.shape[1] // NOPE
    groups = heads // GROUP
    n_keys = CTX * n_rows
    n_chunks = (model_dim // 2 // COL_BLK) * (n_rows // PIECE)
    bf16, f32 = jnp.bfloat16, jnp.float32
    vmem = pl.BlockSpec(memory_space=pltpu.VMEM)
    hbm = pl.BlockSpec(memory_space=pl.ANY)
    dma = pltpu.SemaphoreType.DMA
    return pl.pallas_call(
        layer_kernel,
        out_shape=jax.ShapeDtypeStruct((n_rows, model_dim), bf16),
        in_specs=[hbm, vmem, vmem, vmem, vmem] + [hbm] * 8,
        out_specs=vmem,
        scratch_shapes=[
            pltpu.VMEM((n_rows, model_dim), bf16),
            pltpu.VMEM((ROPE, model_dim), bf16),
            pltpu.VMEM((O_SLOTS, model_dim, DOWN_BLK), bf16),
            pltpu.VMEM((2, q_rank, GROUP * NOPE), bf16),
            pltpu.VMEM((2, q_rank, GROUP * ROPE), bf16),
            pltpu.VMEM((2, 2, lat_rank, GROUP * NOPE), bf16),
            pltpu.VMEM((n_rows, GROUP * ROPE), f32),
            pltpu.VMEM((n_rows, GROUP * ROPE), f32),
            pltpu.VMEM((2, CTX, PIECE, lat_rank + 2 * ROPE), bf16),
            pltpu.VMEM((2, n_keys, 2 * ROPE), bf16),
            pltpu.VMEM((n_rows, q_rank), f32),
            pltpu.VMEM((n_rows, q_rank), bf16),
            pltpu.VMEM((groups, PIECE, GROUP * NOPE), bf16),
            pltpu.VMEM((groups, PIECE, GROUP * ROPE), bf16),
            pltpu.VMEM((groups, 2, n_keys // 2, GROUP * NOPE), bf16),
            pltpu.VMEM((PIECE, n_keys // 2 + n_keys), f32),
            pltpu.VMEM((n_rows, heads * VALUE), bf16),
            pltpu.VMEM((2, n_chunks, PIECE, COL_BLK), f32),
            pltpu.VMEM((2, n_chunks, PIECE, COL_BLK), f32),
            dma, dma, dma((2,)), dma((2, 2)), dma((2, 2)), dma((O_SLOTS, 2)),
            dma((3,)), dma((3,)),
            dma((2, n_chunks)), dma((2, n_chunks)), dma((2, n_chunks)), dma((2, n_chunks)),
        ],
        compiler_params=pltpu.CompilerParams(collective_id=0, has_side_effects=True, vmem_limit_bytes=67043328),
        name='layer',
    )(tok_x, tok_pos, jnp.asarray(inv_freq_row()), g_q, g_kv, w_dq, w_uq, w_qr, w_dkv, w_kr.T, w_uk, w_uv, w_o)


def solution(mesh):
    tok_spec = P(('dp', 'ctx'), None)
    pos_spec = P(('dp', 'ctx'))
    full_mat = P(None, None)
    full_vec = P(None)
    col_spec = P(None, 'tp')
    row_spec = P('tp', None)
    return jax.shard_map(layer, mesh=mesh,
                         in_specs=(tok_spec, pos_spec, full_mat, full_vec, col_spec, col_spec, full_mat, full_vec, full_mat, col_spec, col_spec, row_spec),
                         out_specs=tok_spec, check_vma=False)
```

time: 166 us -> 157 us (0.946)
  local copies, waits for them, and re-layouts: 8.97 us -> 3.4 us
  other arithmetic: 2.5 us -> 0 us
    unnamed x2 -> x1, local copies, waits for them, and re-layouts: 5.71 us -> 3.4 us
    concatenate x2 -> x0, local copies, waits for them, and re-layouts: 1.99 us -> none  [the longest x1 1 us: rope_tables(): jnp.concatenate([-sin_t, sin_t] * copies, axis=-1)]
where the time goes in v4:
time: 157 us
  Pallas kernels  153 us (97%)
  local copies, waits for them, and re-layouts  3.4 us (2%)
    pallas_call x1, Pallas kernels, layer(): pl.pallas_call(layer_kernel, out_shape=jax.ShapeDtypeStruct((n_rows, mode...  153 us
    unnamed x1, local copies, waits for them, and re-layouts  3.4 us

profile of v4, /device:TPU:0, one launch (start us, length us, event | category | flops | bytes accessed | tf_op | source)
XLA Modules:
  0.0 156.7 jit_solution(2881446267008269858)
XLA Ops:
  0.0 153.3 %layer.1 = bf16[256,5120]{1,0:T(8,128)(2,1)} custom-call(bf16[256,5120]{1,0:T(8,128)(2,1)} %x_hbm.1, s32[256]{0:T(256)} %pos_ref.1, f32[1,128]{1,0:T(1,128)} %constant.2.clone.freq_ref, bf16[1536]{0:T(1024)(128)(2,1)} %gq_ref.1, bf16[512]{0:T(512)(128)(2,1)} %gkv_ref.1, bf16[5120,1536]{1,0:T(8,128)(2,1)} %wdq_hbm.1, bf16[1536,4096]{1,0:T(8,128)(2,1)} %wuq_hbm.1, ...), custom_call_target="tpu_custom_call" | custom-call | tf_op jit(solution)/shard_map/layer/pallas_call | solution.py:441
  153.3 3.4 %copy.15 = bf16[256,5120]{1,0:T(8,128)(2,1)} copy(bf16[256,5120]{1,0:T(8,128)(2,1)} %layer.1) | data formatting | bytes 5242880

commit v5 on v4

--- a/solution.py
+++ b/solution.py
@@ -25,8 +25,12 @@
 LOW_FIRST = 4
 HIGH_FIRST = 5
 EVENTS_OUT = 3
+RELAY_AT = 5
+EXTRA = 2
+LOW_WIDE = 4
+HIGH_WIDE = 2
 SUM_LAG = 2
-BACK_LAG = 3
+BACK_LAG = (2, 3)
 MESH_ID = pl.DeviceIdType.MESH
 
 
@@ -50,11 +54,11 @@
 
 
 def layer_kernel(x_hbm, pos_ref, freq_ref, gq_ref, gkv_ref, wdq_hbm, wuq_hbm, wqr_hbm, wdkv_hbm, wkr_hbm, wuk_hbm, wuv_hbm, wo_hbm,
-                 y_ref,
-                 x_ref, wkr_ref, wbig, wq, wqr, wkv,
+                 y_hbm,
+                 y_ref, x_ref, wkr_ref, wbig, wq, wqr, wkv,
                  cos_ref, sin_ref, lat, kpe, cq_f, cq, qn, qp, kv_low, cap, o_ref, acc, rbuf,
                  x_sem, kr_sem, down_sem, q_sem, kv_sem, o_sem,
-                 lat_send, lat_recv, f_send, f_recv, b_send, b_recv):
+                 lat_send, lat_recv, f_send, f_recv, b_send, b_recv, y_sem):
     my_tp = lax.axis_index('tp')
     my_ctx = lax.axis_index('ctx')
     n_rows, n_cols = y_ref.shape
@@ -75,7 +79,7 @@
 
     def dq_copy(blk):
         cols = pl.ds(pl.multiple_of((blk - 1) * DOWN_BLK, DOWN_BLK), DOWN_BLK)
-        slot = lax.rem(blk, 2)
+        slot = lax.rem(blk, O_SLOTS)
         return pltpu.make_async_copy(wdq_hbm.at[:, cols], wbig.at[slot], down_sem.at[slot])
 
     dkv_copy = pltpu.make_async_copy(wdkv_hbm, wbig.at[0], down_sem.at[0])
@@ -116,6 +120,7 @@
     kr_copy.start()
     dkv_copy.start()
     dq_copy(1).start()
+    dq_copy(2).start()
 
     barrier = pltpu.get_barrier_semaphore()
     for peer in (partner, across):
@@ -177,30 +182,42 @@
     lat_copy(my_ctx, across, 1).start()
     lat_copy(my_ctx, partner, 0).start()
 
+    for blk in range(O_SLOTS, n_down):
+        dq_copy(blk).start()
+    for grp in range(2):
+        start_all(q_copies(grp))
+
     def dq_step(blk, _):
-        @pl.when(blk + 1 < n_down)
-        def _():
-            dq_copy(blk + 1).start()
-
-        @pl.when(blk + 1 == n_down)
-        def _():
-            for grp in range(2):
-                start_all(q_copies(grp))
-                start_all(kv_copies(grp))
-
         dq_copy(blk).wait()
         cols = pl.ds(pl.multiple_of((blk - 1) * DOWN_BLK, DOWN_BLK), DOWN_BLK)
-        cq_f[:, cols] = jnp.dot(x_ref[...], wbig[lax.rem(blk, 2)], preferred_element_type=jnp.float32)
+        cq_f[:, cols] = jnp.dot(x_ref[...], wbig[lax.rem(blk, O_SLOTS)], preferred_element_type=jnp.float32)
         return 0
 
     lax.fori_loop(1, n_down, dq_step, 0)
     cq[...] = rms_norm(cq_f[...], gq_ref[...].astype(jnp.float32).reshape(1, q_rank)).astype(jnp.bfloat16)
 
-    for turn in range(O_SLOTS - 1):
-        start_all(o_copies(turn))
-
-    lat_copy(across, across, 1).wait_recv()
-    lat_copy(across, partner, 2).start()
+    def q_step(grp, _):
+        slot = lax.rem(grp, 2)
+        wait_all(q_copies(grp))
+        qn[grp] = jnp.dot(cq[...], wq[slot], preferred_element_type=jnp.float32).astype(jnp.bfloat16)
+        q_rot = jnp.dot(cq[...], wqr[slot], preferred_element_type=jnp.float32)
+        qp[grp] = rotate(q_rot, cos_ref[...], sin_ref[...]).astype(jnp.bfloat16)
+
+        @pl.when(grp + 2 < groups)
+        def _():
+            start_all(q_copies(grp + 2))
+
+        @pl.when(grp + 2 >= groups)
+        def _():
+            start_all(kv_copies(grp + 2 - groups))
+
+        @pl.when(grp == RELAY_AT)
+        def _():
+            lat_copy(across, across, 1).wait_recv()
+            lat_copy(across, partner, 2).start()
+        return 0
+
+    lax.fori_loop(0, groups, q_step, 0)
     lat_copy(partner, partner, 0).wait_recv()
     lat_copy(across, partner, 2).wait_recv()
 
@@ -212,16 +229,20 @@
 
     expo_scale = (NOPE + ROPE) ** -0.5 * math.log2(math.e)
 
-    def attend(q_nope, q_rot, keys, k_rots, values, caps):
-        k_cat = jnp.concatenate([keys, k_rots], axis=1)
-        q_cat = jnp.concatenate([q_nope, q_rot], axis=1)
-        scores = lax.dot_general(q_cat, k_cat, (((1,), (1,)), ((), ())), preferred_element_type=jnp.float32)
-        scores = jnp.minimum(scores, caps)
-        top = jnp.max(scores, axis=-1, keepdims=True)
-        prob = jnp.exp2((scores - top) * expo_scale)
-        total = jnp.sum(prob, axis=-1, keepdims=True)
-        out = jnp.dot(prob.astype(jnp.bfloat16), values, preferred_element_type=jnp.float32)
-        return (out / total).astype(jnp.bfloat16)
+    def attend(jobs):
+        scores = [jnp.minimum(lax.dot_general(q_cat, k_cat, (((1,), (1,)), ((), ())), preferred_element_type=jnp.float32), caps)
+                  for q_cat, k_cat, _, caps, _ in jobs]
+        tops = [jnp.max(score, axis=-1, keepdims=True) for score in scores]
+        probs = [jnp.exp2((score - top) * expo_scale) for score, top in zip(scores, tops)]
+        totals = [jnp.sum(prob, axis=-1, keepdims=True) for prob in probs]
+        outs = [jnp.dot(prob.astype(jnp.bfloat16), job[2], preferred_element_type=jnp.float32) for prob, job in zip(probs, jobs)]
+        for out, total, job in zip(outs, totals, jobs):
+            rows, cols = job[4]
+            o_ref[rows, cols] = (out / total).astype(jnp.bfloat16)
+
+    def queries(grp, head, rows):
+        pair = slice((head // 2) * 2 * ROPE, (head // 2 + 1) * 2 * ROPE)
+        return jnp.concatenate([qn[grp, rows, head * NOPE:(head + 1) * NOPE], qp[grp, rows, pair]], axis=1)
 
     def up_project(half, slot):
         rows = lat[half, :, :, :lat_rank].reshape(low_keys, lat_rank)
@@ -230,29 +251,26 @@
     def out_cols(grp, head):
         return pl.ds(pl.multiple_of(grp * (GROUP * VALUE), GROUP * VALUE) + head * VALUE, VALUE)
 
+    low, high = slice(0, PIECE), slice(PIECE, 2 * PIECE)
+
     def low_step(grp, _):
         slot = lax.rem(grp, 2)
-        wait_all(q_copies(grp))
         wait_all(kv_copies(grp))
-        q_nope = jnp.dot(cq[...], wq[slot], preferred_element_type=jnp.float32).astype(jnp.bfloat16)
-        q_rot = jnp.dot(cq[...], wqr[slot], preferred_element_type=jnp.float32)
-        q_rot = rotate(q_rot, cos_ref[...], sin_ref[...]).astype(jnp.bfloat16)
-        qn[grp] = q_nope[PIECE:]
-        qp[grp] = q_rot[PIECE:]
         k_low, v_low = up_project(0, slot)
         kv_low[grp, 0] = k_low
         kv_low[grp, 1] = v_low
+        jobs = []
         for head in range(GROUP):
             cols = slice(head * NOPE, (head + 1) * NOPE)
-            pair = slice((head // 2) * 2 * ROPE, (head // 2 + 1) * 2 * ROPE)
-            o_ref[:PIECE, out_cols(grp, head)] = attend(
-                q_nope[:PIECE, cols], q_rot[:PIECE, pair], k_low[:, cols], kpe[head % 2, :low_keys], v_low[:, cols], cap[:, :low_keys])
-
+            k_cat = jnp.concatenate([k_low[:, cols], kpe[head % 2, :low_keys]], axis=1)
+            jobs.append((queries(grp, head, low), k_cat, v_low[:, cols], cap[:, :low_keys], (low, out_cols(grp, head))))
+        for first in range(0, GROUP, LOW_WIDE):
+            attend(jobs[first:first + LOW_WIDE])
         start_all(kv_copies(grp + 2))
 
-        @pl.when(grp + 2 < groups)
-        def _():
-            start_all(q_copies(grp + 2))
+        @pl.when((grp >= 1) & (grp < O_SLOTS))
+        def _():
+            start_all(o_copies(grp - 1))
         return 0
 
     lax.fori_loop(0, groups, low_step, 0)
@@ -261,13 +279,15 @@
         slot = lax.rem(grp, 2)
         wait_all(kv_copies(groups + grp))
         k_up, v_up = up_project(1, slot)
+        jobs = []
         for head in range(GROUP):
             cols = slice(head * NOPE, (head + 1) * NOPE)
-            pair = slice((head // 2) * 2 * ROPE, (head // 2 + 1) * 2 * ROPE)
             keys = jnp.concatenate([kv_low[grp, 0, :, cols], k_up[:, cols]], axis=0)
             values = jnp.concatenate([kv_low[grp, 1, :, cols], v_up[:, cols]], axis=0)
-            o_ref[PIECE:, out_cols(grp, head)] = attend(
-                qn[grp, :, cols], qp[grp, :, pair], keys, kpe[head % 2], values, cap[:, low_keys:])
+            k_cat = jnp.concatenate([keys, kpe[head % 2]], axis=1)
+            jobs.append((queries(grp, head, high), k_cat, values, cap[:, low_keys:], (high, out_cols(grp, head))))
+        for first in range(0, GROUP, HIGH_WIDE):
+            attend(jobs[first:first + HIGH_WIDE])
 
         @pl.when(grp + 2 < groups)
         def _():
@@ -295,6 +315,9 @@
             send_sem=b_send.at[side, chunk], recv_sem=b_recv.at[side, chunk],
             device_id={'tp': back[side]}, device_id_type=MESH_ID)
 
+    def y_copy(side, chunk):
+        return pltpu.make_async_copy(y_ref.at[y_slice(side, chunk)], y_hbm.at[y_slice(side, chunk)], y_sem.at[side, chunk])
+
     def reduce_event(side, event, row):
         chunk = event - SUM_LAG * (depth[side] - 1)
         live = (chunk >= 0) & (chunk < col_steps)
@@ -314,9 +337,10 @@
             total = acc[side, chunk] + rbuf[side, chunk]
             y_ref[y_slice(side, chunk)] = total.astype(y_ref.dtype)
             b_copy(side, chunk).start()
+            y_copy(side, chunk).start()
 
     def back_event(side, event, row):
-        chunk = event - BACK_LAG * (TP - 2 - depth[side])
+        chunk = event - BACK_LAG[row] * (TP - 2 - depth[side])
         live = (chunk >= 0) & (chunk < col_steps)
         chunk = chunk + row * col_steps
 
@@ -327,6 +351,10 @@
         @pl.when(live & (depth[side] > 0) & (depth[side] < TP - 1))
         def _():
             b_copy(side, chunk).start()
+
+        @pl.when(live & (depth[side] < TP - 1))
+        def _():
+            y_copy(side, chunk).start()
 
     def both(event_fn, event, row):
         for side in range(2):
@@ -349,7 +377,7 @@
                 f_copy(side, turn).start()
 
     sum_events = col_steps + SUM_LAG * (TP - 2)
-    back_events = col_steps + BACK_LAG * (TP - 2)
+    back_events = [col_steps + lag * (TP - 2) for lag in BACK_LAG]
 
     def low_out(step, _):
         project(0, step)
@@ -380,34 +408,34 @@
         def _():
             both(reduce_event, first_sum + step // 2, 0)
 
-        @pl.when(step >= HIGH_FIRST)
-        def _():
-            both(back_event, step - HIGH_FIRST, 0)
+        @pl.when((step >= HIGH_FIRST) & (lax.rem(step, 2) == 1))
+        def _():
+            both(back_event, (step - HIGH_FIRST) // 2, 0)
         return 0
 
     lax.fori_loop(0, col_steps, high_out, 0)
 
-    first_back = col_steps - HIGH_FIRST
-    for event in range(first_sum + (col_steps + 1) // 2, sum_events):
-        both(reduce_event, event, 0)
+    first_back = (col_steps - HIGH_FIRST + 1) // 2
 
     def high_sum(event, _):
+        @pl.when(lax.rem(event, 2) == 1)
+        def _():
+            both(back_event, first_back + EXTRA + event // 2, 0)
+
         both(reduce_event, event, 1)
-
-        @pl.when(first_back + event < back_events)
-        def _():
-            both(back_event, first_back + event, 0)
-        return 0
-
+        return 0
+
+    for event in range(EXTRA):
+        both(back_event, first_back + event, 0)
     lax.fori_loop(0, sum_events, high_sum, 0)
-    for event in range(first_back + sum_events, back_events):
+    for event in range(first_back + EXTRA + sum_events // 2, back_events[0]):
         both(back_event, event, 0)
 
     def high_back(event, _):
         both(back_event, event, 1)
         return 0
 
-    lax.fori_loop(0, back_events, high_back, 0)
+    lax.fori_loop(0, back_events[1], high_back, 0)
 
     lat_copy(my_ctx, partner, 0).wait_send()
     lat_copy(my_ctx, across, 1).wait_send()
@@ -422,6 +450,8 @@
             @pl.when(depth[side] > 0)
             def _():
                 b_copy(side, chunk).wait_send()
+
+            y_copy(side, chunk).wait()
         return 0
 
     lax.fori_loop(0, n_chunks, drain, 0)
@@ -442,8 +472,9 @@
         layer_kernel,
         out_shape=jax.ShapeDtypeStruct((n_rows, model_dim), bf16),
         in_specs=[hbm, vmem, vmem, vmem, vmem] + [hbm] * 8,
-        out_specs=vmem,
+        out_specs=hbm,
         scratch_shapes=[
+            pltpu.VMEM((n_rows, model_dim), bf16),
             pltpu.VMEM((n_rows, model_dim), bf16),
             pltpu.VMEM((ROPE, model_dim), bf16),
             pltpu.VMEM((O_SLOTS, model_dim, DOWN_BLK), bf16),
@@ -456,16 +487,16 @@
             pltpu.VMEM((2, n_keys, 2 * ROPE), bf16),
             pltpu.VMEM((n_rows, q_rank), f32),
             pltpu.VMEM((n_rows, q_rank), bf16),
-            pltpu.VMEM((groups, PIECE, GROUP * NOPE), bf16),
-            pltpu.VMEM((groups, PIECE, GROUP * ROPE), bf16),
+            pltpu.VMEM((groups, n_rows, GROUP * NOPE), bf16),
+            pltpu.VMEM((groups, n_rows, GROUP * ROPE), bf16),
             pltpu.VMEM((groups, 2, n_keys // 2, GROUP * NOPE), bf16),
             pltpu.VMEM((PIECE, n_keys // 2 + n_keys), f32),
             pltpu.VMEM((n_rows, heads * VALUE), bf16),
             pltpu.VMEM((2, n_chunks, PIECE, COL_BLK), f32),
             pltpu.VMEM((2, n_chunks, PIECE, COL_BLK), f32),
-            dma, dma, dma((2,)), dma((2, 2)), dma((2, 2)), dma((O_SLOTS, 2)),
+            dma, dma, dma((O_SLOTS,)), dma((2, 2)), dma((2, 2)), dma((O_SLOTS, 2)),
             dma((3,)), dma((3,)),
-            dma((2, n_chunks)), dma((2, n_chunks)), dma((2, n_chunks)), dma((2, n_chunks)),
+            dma((2, n_chunks)), dma((2, n_chunks)), dma((2, n_chunks)), dma((2, n_chunks)), dma((2, n_chunks)),
         ],
         compiler_params=pltpu.CompilerParams(collective_id=0, has_side_effects=True, vmem_limit_bytes=67043328),
         name='layer',

time: 157 us -> 147 us (0.936)
  Pallas kernels: 153 us -> 143 us
    pallas_call x1, Pallas kernels: 153 us -> 143 us  [layer(): pl.pallas_call(layer_kernel, out_shape=jax.ShapeDtypeStruct((n_rows, mode...]
where the time goes in v5:
time: 147 us
  Pallas kernels  143 us (97%)
  local copies, waits for them, and re-layouts  3.4 us (2%)
    pallas_call x1, Pallas kernels, layer(): pl.pallas_call(layer_kernel, out_shape=jax.ShapeDtypeStruct((n_rows, mode...  143 us
    unnamed x1, local copies, waits for them, and re-layouts  3.4 us

profile of v5, /device:TPU:0, one launch (start us, length us, event | category | flops | bytes accessed | tf_op | source)
XLA Modules:
  0.0 146.8 jit_solution(9082105365397808602)
XLA Ops:
  0.0 143.4 %layer.1 = bf16[256,5120]{1,0:T(8,128)(2,1)} custom-call(bf16[256,5120]{1,0:T(8,128)(2,1)} %x_hbm.1, s32[256]{0:T(256)} %pos_ref.1, f32[1,128]{1,0:T(1,128)} %constant.2.clone.freq_ref, bf16[1536]{0:T(1024)(128)(2,1)} %gq_ref.1, bf16[512]{0:T(512)(128)(2,1)} %gkv_ref.1, bf16[5120,1536]{1,0:T(8,128)(2,1)} %wdq_hbm.1, bf16[1536,4096]{1,0:T(8,128)(2,1)} %wuq_hbm.1, ...), custom_call_target="tpu_custom_call" | custom-call | tf_op jit(solution)/shard_map/layer/pallas_call | solution.py:471
  143.4 3.4 %copy.15 = bf16[256,5120]{1,0:T(8,128)(2,1)} copy(bf16[256,5120]{1,0:T(8,128)(2,1)} %layer.1) | data formatting | bytes 5242880

commit v6 on v5

--- a/solution.py
+++ b/solution.py
@@ -25,12 +25,13 @@
 LOW_FIRST = 4
 HIGH_FIRST = 5
 EVENTS_OUT = 3
-RELAY_AT = 5
-EXTRA = 2
-LOW_WIDE = 4
+RELAY_AT = 1
+Q_AHEAD = 3
+O_AT = 3
+EXTRA = 0
 HIGH_WIDE = 2
 SUM_LAG = 2
-BACK_LAG = (2, 3)
+BACK_LAG = (1, 3)
 MESH_ID = pl.DeviceIdType.MESH
 
 
@@ -119,8 +120,6 @@
     x_copy.start()
     kr_copy.start()
     dkv_copy.start()
-    dq_copy(1).start()
-    dq_copy(2).start()
 
     barrier = pltpu.get_barrier_semaphore()
     for peer in (partner, across):
@@ -156,10 +155,12 @@
 
     x_copy.wait()
     kr_copy.wait()
+    dq_copy(1).start()
     rot = lax.dot_general(x_ref[...], wkr_ref[...], (((1,), (1,)), ((), ())), preferred_element_type=jnp.float32)
     rot = jnp.concatenate([rot, rot], axis=1)
     k_rot = rotate(rot, cos_ref[:, :2 * ROPE], sin_ref[:, :2 * ROPE]).astype(jnp.bfloat16)
     dkv_copy.wait()
+    dq_copy(2).start()
     c_kv = rms_norm(jnp.dot(x_ref[...], wbig[0], preferred_element_type=jnp.float32), gkv_ref[...].astype(jnp.float32).reshape(1, lat_rank)).astype(jnp.bfloat16)
     for half in range(2):
         rows = slice(half * PIECE, (half + 1) * PIECE)
@@ -196,20 +197,20 @@
     lax.fori_loop(1, n_down, dq_step, 0)
     cq[...] = rms_norm(cq_f[...], gq_ref[...].astype(jnp.float32).reshape(1, q_rank)).astype(jnp.bfloat16)
 
-    def q_step(grp, _):
+    def q_project(grp):
         slot = lax.rem(grp, 2)
-        wait_all(q_copies(grp))
         qn[grp] = jnp.dot(cq[...], wq[slot], preferred_element_type=jnp.float32).astype(jnp.bfloat16)
         q_rot = jnp.dot(cq[...], wqr[slot], preferred_element_type=jnp.float32)
         qp[grp] = rotate(q_rot, cos_ref[...], sin_ref[...]).astype(jnp.bfloat16)
 
-        @pl.when(grp + 2 < groups)
-        def _():
-            start_all(q_copies(grp + 2))
-
-        @pl.when(grp + 2 >= groups)
-        def _():
-            start_all(kv_copies(grp + 2 - groups))
+    def q_step(grp, _):
+        wait_all(q_copies(grp))
+        q_project(grp)
+        start_all(q_copies(grp + 2))
+
+        @pl.when(grp < 2)
+        def _():
+            start_all(kv_copies(grp))
 
         @pl.when(grp == RELAY_AT)
         def _():
@@ -217,7 +218,7 @@
             lat_copy(across, partner, 2).start()
         return 0
 
-    lax.fori_loop(0, groups, q_step, 0)
+    lax.fori_loop(0, Q_AHEAD, q_step, 0)
     lat_copy(partner, partner, 0).wait_recv()
     lat_copy(across, partner, 2).wait_recv()
 
@@ -229,9 +230,10 @@
 
     expo_scale = (NOPE + ROPE) ** -0.5 * math.log2(math.e)
 
-    def attend(jobs):
+    def attend(jobs, between):
         scores = [jnp.minimum(lax.dot_general(q_cat, k_cat, (((1,), (1,)), ((), ())), preferred_element_type=jnp.float32), caps)
                   for q_cat, k_cat, _, caps, _ in jobs]
+        between()
         tops = [jnp.max(score, axis=-1, keepdims=True) for score in scores]
         probs = [jnp.exp2((score - top) * expo_scale) for score, top in zip(scores, tops)]
         totals = [jnp.sum(prob, axis=-1, keepdims=True) for prob in probs]
@@ -253,9 +255,11 @@
 
     low, high = slice(0, PIECE), slice(PIECE, 2 * PIECE)
 
-    def low_step(grp, _):
+    def low_step(grp, ahead):
         slot = lax.rem(grp, 2)
         wait_all(kv_copies(grp))
+        if ahead:
+            wait_all(q_copies(grp + Q_AHEAD))
         k_low, v_low = up_project(0, slot)
         kv_low[grp, 0] = k_low
         kv_low[grp, 1] = v_low
@@ -264,16 +268,27 @@
             cols = slice(head * NOPE, (head + 1) * NOPE)
             k_cat = jnp.concatenate([k_low[:, cols], kpe[head % 2, :low_keys]], axis=1)
             jobs.append((queries(grp, head, low), k_cat, v_low[:, cols], cap[:, :low_keys], (low, out_cols(grp, head))))
-        for first in range(0, GROUP, LOW_WIDE):
-            attend(jobs[first:first + LOW_WIDE])
+        attend(jobs, (lambda: q_project(grp + Q_AHEAD)) if ahead else (lambda: None))
         start_all(kv_copies(grp + 2))
-
-        @pl.when((grp >= 1) & (grp < O_SLOTS))
-        def _():
-            start_all(o_copies(grp - 1))
-        return 0
-
-    lax.fori_loop(0, groups, low_step, 0)
+        if ahead:
+            @pl.when(grp + Q_AHEAD + 2 < groups)
+            def _():
+                start_all(q_copies(grp + Q_AHEAD + 2))
+
+        @pl.when((grp >= O_AT) & (grp < O_AT + O_SLOTS - 1))
+        def _():
+            start_all(o_copies(grp - O_AT))
+
+    def low_ahead(grp, _):
+        low_step(grp, True)
+        return 0
+
+    def low_rest(grp, _):
+        low_step(grp, False)
+        return 0
+
+    lax.fori_loop(0, groups - Q_AHEAD, low_ahead, 0)
+    lax.fori_loop(groups - Q_AHEAD, groups, low_rest, 0)
 
     def high_step(grp):
         slot = lax.rem(grp, 2)
@@ -287,7 +302,7 @@
             k_cat = jnp.concatenate([keys, kpe[head % 2]], axis=1)
             jobs.append((queries(grp, head, high), k_cat, values, cap[:, low_keys:], (high, out_cols(grp, head))))
         for first in range(0, GROUP, HIGH_WIDE):
-            attend(jobs[first:first + HIGH_WIDE])
+            attend(jobs[first:first + HIGH_WIDE], lambda: None)
 
         @pl.when(grp + 2 < groups)
         def _():

time: 147 us -> 144 us (0.980)
  Pallas kernels: 143 us -> 140 us
    pallas_call x1, Pallas kernels: 143 us -> 140 us  [layer(): pl.pallas_call(layer_kernel, out_shape=jax.ShapeDtypeStruct((n_rows, mode...]
where the time goes in v6:
time: 144 us
  Pallas kernels  140 us (97%)
  local copies, waits for them, and re-layouts  3.4 us (2%)
    pallas_call x1, Pallas kernels, layer(): pl.pallas_call(layer_kernel, out_shape=jax.ShapeDtypeStruct((n_rows, mode...  140 us
    unnamed x1, local copies, waits for them, and re-layouts  3.4 us

profile of v6, /device:TPU:0, one launch (start us, length us, event | category | flops | bytes accessed | tf_op | source)
XLA Modules:
  0.0 143.5 jit_solution(5826503670271088803)
XLA Ops:
  0.0 140.1 %layer.1 = bf16[256,5120]{1,0:T(8,128)(2,1)} custom-call(bf16[256,5120]{1,0:T(8,128)(2,1)} %x_hbm.1, s32[256]{0:T(256)} %pos_ref.1, f32[1,128]{1,0:T(1,128)} %constant.2.clone.freq_ref, bf16[1536]{0:T(1024)(128)(2,1)} %gq_ref.1, bf16[512]{0:T(512)(128)(2,1)} %gkv_ref.1, bf16[5120,1536]{1,0:T(8,128)(2,1)} %wdq_hbm.1, bf16[1536,4096]{1,0:T(8,128)(2,1)} %wuq_hbm.1, ...), custom_call_target="tpu_custom_call" | custom-call | tf_op jit(solution)/shard_map/layer/pallas_call | solution.py:486
  140.1 3.4 %copy.15 = bf16[256,5120]{1,0:T(8,128)(2,1)} copy(bf16[256,5120]{1,0:T(8,128)(2,1)} %layer.1) | data formatting | bytes 5242880

commit v7 on v6

--- a/solution.py
+++ b/solution.py
@@ -15,6 +15,7 @@
 TP = 4
 CTX = 4
 PIECE = 128
+SPLIT = 1
 NOPE = 128
 ROPE = 64
 VALUE = 128
@@ -28,10 +29,11 @@
 RELAY_AT = 1
 Q_AHEAD = 3
 O_AT = 3
+STORE_SLABS = 8
 EXTRA = 0
 HIGH_WIDE = 2
-SUM_LAG = 2
-BACK_LAG = (1, 3)
+SUM_LAG = 3
+BACK_LAG = (1, 4)
 MESH_ID = pl.DeviceIdType.MESH
 
 
@@ -101,7 +103,9 @@
     row_blks = n_rows // PIECE
     half_cols = n_cols // 2
     col_steps = half_cols // COL_BLK
-    n_chunks = col_steps * row_blks
+    n_chunks = col_steps * row_blks * SPLIT
+    row_chunks = col_steps * SPLIT
+    chunk_rows = PIECE // SPLIT
 
     def o_copies(turn):
         step, slot = lax.rem(turn, col_steps), lax.rem(turn, O_SLOTS)
@@ -313,8 +317,9 @@
     back = (right, left)
 
     def y_slice(side, chunk):
-        row, step = chunk // col_steps, lax.rem(chunk, col_steps)
-        return (pl.ds(pl.multiple_of(row * PIECE, PIECE), PIECE),
+        row, within = chunk // row_chunks, lax.rem(chunk, row_chunks)
+        step, part = within // SPLIT, lax.rem(within, SPLIT)
+        return (pl.ds(pl.multiple_of(row * PIECE + part * chunk_rows, chunk_rows), chunk_rows),
                 pl.ds(pl.multiple_of(side * half_cols + step * COL_BLK, COL_BLK), COL_BLK))
 
     def f_copy(side, chunk):
@@ -335,8 +340,8 @@
 
     def reduce_event(side, event, row):
         chunk = event - SUM_LAG * (depth[side] - 1)
-        live = (chunk >= 0) & (chunk < col_steps)
-        chunk = chunk + row * col_steps
+        live = (chunk >= 0) & (chunk < row_chunks)
+        chunk = chunk + row * row_chunks
 
         @pl.when(live & (depth[side] > 0))
         def _():
@@ -356,8 +361,8 @@
 
     def back_event(side, event, row):
         chunk = event - BACK_LAG[row] * (TP - 2 - depth[side])
-        live = (chunk >= 0) & (chunk < col_steps)
-        chunk = chunk + row * col_steps
+        live = (chunk >= 0) & (chunk < row_chunks)
+        chunk = chunk + row * row_chunks
 
         @pl.when(live & (depth[side] < TP - 1))
         def _():
@@ -372,8 +377,9 @@
             y_copy(side, chunk).start()
 
     def both(event_fn, event, row):
-        for side in range(2):
-            event_fn(side, event, row)
+        for part in range(SPLIT):
+            for side in range(2):
+                event_fn(side, event * SPLIT + part, row)
 
     def project(row, step):
         turn = row * col_steps + step
@@ -384,15 +390,17 @@
 
         wait_all(o_copies(turn))
         part = jnp.dot(o_ref[row * PIECE:(row + 1) * PIECE], wbig[lax.rem(turn, O_SLOTS), :heads * VALUE], preferred_element_type=jnp.float32)
-        for side in range(2):
-            acc[side, turn] = part[:, side * COL_BLK:(side + 1) * COL_BLK]
-
-            @pl.when(depth[side] == 0)
-            def _():
-                f_copy(side, turn).start()
-
-    sum_events = col_steps + SUM_LAG * (TP - 2)
-    back_events = [col_steps + lag * (TP - 2) for lag in BACK_LAG]
+        for half in range(SPLIT):
+            for side in range(2):
+                chunk = turn * SPLIT + half
+                acc[side, chunk] = part[half * chunk_rows:(half + 1) * chunk_rows, side * COL_BLK:(side + 1) * COL_BLK]
+
+                @pl.when(depth[side] == 0)
+                def _():
+                    f_copy(side, chunk).start()
+
+    sum_events = pl.cdiv(row_chunks + SUM_LAG * (TP - 2), SPLIT)
+    back_events = [pl.cdiv(row_chunks + lag * (TP - 2), SPLIT) for lag in BACK_LAG]
 
     def low_out(step, _):
         project(0, step)
@@ -440,6 +448,8 @@
         both(reduce_event, event, 1)
         return 0
 
+    for event in range(first_sum + col_steps // 2, sum_events):
+        both(reduce_event, event, 0)
     for event in range(EXTRA):
         both(back_event, first_back + event, 0)
     lax.fori_loop(0, sum_events, high_sum, 0)
@@ -470,6 +480,33 @@
         return 0
 
     lax.fori_loop(0, n_chunks, drain, 0)
+
+
+def store_kernel(src_hbm, dst_hbm, slab, in_sem, out_sem):
+    rows = src_hbm.shape[0] // STORE_SLABS
+    parts = [pl.ds(part * rows, rows) for part in range(STORE_SLABS)]
+    loads = [pltpu.make_async_copy(src_hbm.at[part], slab.at[part], in_sem.at[idx]) for idx, part in enumerate(parts)]
+    stores = [pltpu.make_async_copy(slab.at[part], dst_hbm.at[part], out_sem.at[idx]) for idx, part in enumerate(parts)]
+    for load in loads:
+        load.start()
+    for load, store in zip(loads, stores):
+        load.wait()
+        store.start()
+    for store in stores:
+        store.wait()
+
+
+def store_rows(rows):
+    hbm = pl.BlockSpec(memory_space=pl.ANY)
+    dma = pltpu.SemaphoreType.DMA
+    return pl.pallas_call(
+        store_kernel,
+        out_shape=jax.ShapeDtypeStruct(rows.shape, rows.dtype),
+        in_specs=[hbm],
+        out_specs=hbm,
+        scratch_shapes=[pltpu.VMEM(rows.shape, rows.dtype), dma((STORE_SLABS,)), dma((STORE_SLABS,))],
+        name='store_rows',
+    )(rows)
 
 
 def layer(tok_x, tok_pos, w_dq, g_q, w_uq, w_qr, w_dkv, g_kv, w_kr, w_uk, w_uv, w_o):
@@ -478,12 +515,12 @@
     heads = w_uq.shape[1] // NOPE
     groups = heads // GROUP
     n_keys = CTX * n_rows
-    n_chunks = (model_dim // 2 // COL_BLK) * (n_rows // PIECE)
+    n_chunks = (model_dim // 2 // COL_BLK) * (n_rows // PIECE) * SPLIT
     bf16, f32 = jnp.bfloat16, jnp.float32
     vmem = pl.BlockSpec(memory_space=pltpu.VMEM)
     hbm = pl.BlockSpec(memory_space=pl.ANY)
     dma = pltpu.SemaphoreType.DMA
-    return pl.pallas_call(
+    y_rows = pl.pallas_call(
         layer_kernel,
         out_shape=jax.ShapeDtypeStruct((n_rows, model_dim), bf16),
         in_specs=[hbm, vmem, vmem, vmem, vmem] + [hbm] * 8,
@@ -507,8 +544,8 @@
             pltpu.VMEM((groups, 2, n_keys // 2, GROUP * NOPE), bf16),
             pltpu.VMEM((PIECE, n_keys // 2 + n_keys), f32),
             pltpu.VMEM((n_rows, heads * VALUE), bf16),
-            pltpu.VMEM((2, n_chunks, PIECE, COL_BLK), f32),
-            pltpu.VMEM((2, n_chunks, PIECE, COL_BLK), f32),
+            pltpu.VMEM((2, n_chunks, PIECE // SPLIT, COL_BLK), f32),
+            pltpu.VMEM((2, n_chunks, PIECE // SPLIT, COL_BLK), f32),
             dma, dma, dma((O_SLOTS,)), dma((2, 2)), dma((2, 2)), dma((O_SLOTS, 2)),
             dma((3,)), dma((3,)),
             dma((2, n_chunks)), dma((2, n_chunks)), dma((2, n_chunks)), dma((2, n_chunks)), dma((2, n_chunks)),
@@ -516,6 +553,7 @@
         compiler_params=pltpu.CompilerParams(collective_id=0, has_side_effects=True, vmem_limit_bytes=67043328),
         name='layer',
     )(tok_x, tok_pos, jnp.asarray(inv_freq_row()), g_q, g_kv, w_dq, w_uq, w_qr, w_dkv, w_kr.T, w_uk, w_uv, w_o)
+    return store_rows(y_rows)
 
 
 def solution(mesh):

time: 144 us -> 142 us (0.986)
  local copies, waits for them, and re-layouts: 3.4 us -> 0 us
  Pallas kernels: 140 us -> 142 us
    unnamed x1 -> x0, local copies, waits for them, and re-layouts: 3.4 us -> none
    pallas_call x0 -> x1, Pallas kernels: none -> 2.59 us  [store_rows(): pl.pallas_call(store_kernel, out_shape=jax.ShapeDtypeStruct(rows.shape, r...]
where the time goes in v7:
time: 142 us
  Pallas kernels  142 us (100%)
    pallas_call x1, Pallas kernels, layer(): pl.pallas_call(layer_kernel, out_shape=jax.ShapeDtypeStruct((n_rows, mode...  139 us

profile of v7, /device:TPU:0, one launch (start us, length us, event | category | flops | bytes accessed | tf_op | source)
XLA Modules:
  0.0 142.0 jit_solution(12893067436207200351)
XLA Ops:
  0.0 139.4 %layer.1.src_hbm = bf16[256,5120]{1,0:T(8,128)(2,1)} custom-call(bf16[256,5120]{1,0:T(8,128)(2,1)} %x_hbm.1, s32[256]{0:T(256)} %pos_ref.1, f32[1,128]{1,0:T(1,128)} %constant.2.clone.freq_ref, bf16[1536]{0:T(1024)(128)(2,1)} %gq_ref.1, bf16[512]{0:T(512)(128)(2,1)} %gkv_ref.1, bf16[5120,1536]{1,0:T(8,128)(2,1)} %wdq_hbm.1, bf16[1536,4096]{1,0:T(8,128)(2,1)} %wuq_hbm.1, ...), custom_call_target="tpu_custom_call" | custom-call | tf_op jit(solution)/shard_map/layer/pallas_call | solution.py:523
  139.4 2.6 %store_rows.1 = bf16[256,5120]{1,0:T(8,128)(2,1)} custom-call(bf16[256,5120]{1,0:T(8,128)(2,1)} %layer.1.src_hbm), custom_call_target="tpu_custom_call" | custom-call | tf_op jit(solution)/shard_map/store_rows/pallas_call | solution.py:502
